TPU v7x, 256 devices: a whole 4x4x8 slice. The times are simulated.
256 devices in a mesh: dev: 64 (over z, x, core), rep: 4 (over y).
Axes of the slice: x: 4, y: 4, z: 8, core: 2. Of those that a mesh axis runs over, the one named last changes fastest.
Arguments:
- h_zero: bfloat16 [262144, 256], P(('dev', 'rep')), may hold values from 0 to 2
- h_prev: bfloat16 [262144, 256], P(('dev', 'rep')), may hold values from 0 to 2
- hist_a: bfloat16 [262144, 256], P('dev'), may hold values from 0 to 2
- hist_b: bfloat16 [262144, 256], P('dev'), may hold values from 0 to 2
- tile_vals: bfloat16 [2048, 12, 128, 128], P(('dev', 'rep'))
- tile_cols: int32 [2048, 12], P(('dev', 'rep')), may hold values from 0 to 103, as said below
- pull_rows: int32 [256, 64, 128], P(('dev', 'rep')), may hold values from 0 to 4095
- pull_counts: int32 [256, 64], P(('dev', 'rep')), may hold values from 96 to 128, as said below
- weight_two: bfloat16 [256, 256], replicated, may hold values from -0.375 to 0.375
- weight_three: bfloat16 [256, 256], replicated, may hold values from -0.375 to 0.375
- grad_out: bfloat16 [262144, 256], P(('dev', 'rep')), may hold values from -0.046875 to 0.046875
Outputs:
- layer_three: bfloat16 [262144, 256], P(('dev', 'rep'))
- new_history: bfloat16 [262144, 256], P('dev')
- weight_grad: float32 [256, 256], replicated
Inputs may be any that keep to these rules, and one draw needn't show every extreme that they name: `tile_cols`: entry 0 of a row block names one of its device's own 8 blocks; entries 1 to 3 name blocks of the owner's history shard; the other 8 name pulled blocks of consecutive owners modulo 64, and every owner's block is named by some row block of each device. `pull_rows`: entries at slots at or past the block's count are read by no output. `pull_counts`: every device pulls a full block of 128 rows from some owner and a block of exactly 96 rows from another.
All inputs are finite; a program needn't handle non-finite values.
Results may differ from a plain program's by a relative error of at most 0.0034.
Values may be sent and summed in bfloat16 or wider, within the bound.
A program may use at most 128 MiB of HBM per device.

v0:
```python
import math

import jax
import jax.numpy as jnp
from jax import lax
from jax.sharding import Mesh
from jax.sharding import PartitionSpec as P

DEV = ("dev_0", "dev_1", "dev_2")
DEV_REP = ("dev_0", "dev_1", "dev_2", "rep")


restart = 0.1
strength = 0.5


def in_one_piece(arrays, axis, split_dim, concat_dim, along):
    ends, at = ([], 0)
    for a in arrays[:-1]:
        at += a.shape[along]
        ends.append(at)
    both = jnp.concatenate(arrays, axis=along)
    return tuple(
        jnp.split(
            lax.all_to_all(both, axis, split_axis=split_dim, concat_axis=concat_dim, tiled=True),
            ends,
            axis=along,
        )
    )


def in_order(blocks, dim):
    shape = list(blocks.shape[1:])
    shape[dim] *= blocks.shape[0]
    return jnp.moveaxis(blocks, 0, dim).reshape(shape)


def sent_to_all(value, axis):
    copies = jnp.broadcast_to(value, (lax.axis_size(axis), *value.shape))
    return lax.all_to_all(copies, axis, split_axis=0, concat_axis=0, tiled=True)


def gathered_copies(value, axis, dim):
    return in_order(sent_to_all(value, axis), dim)


def rows_for(lines, length):
    spare = -len(lines) % length
    return jnp.pad(lines, [(0, spare)] + [(0, 0)] * (lines.ndim - 1))


def gathered_by_axis(value, axes, dim):
    far, near = axes
    initial = sent_to_all(value, far)
    blocks = jnp.swapaxes(sent_to_all(initial, near), 0, 1)
    return in_order(blocks.reshape(-1, *value.shape), dim)


def cut_along(value, dim, length):
    shape = value.shape
    blocks = value.reshape(*shape[:dim], length, shape[dim] // length, *shape[dim + 1 :])
    return jnp.moveaxis(blocks, dim, 0)


def summed_on_arrival(value, axis, dim):
    length = lax.axis_size(axis)
    blocks = lax.all_to_all(cut_along(value, dim, length), axis, 0, 0, tiled=True)
    return jnp.sum(blocks, axis=0)


def summed_rows(value, axes, dim):
    far, near = axes
    blocks = cut_along(value, dim, lax.axis_size(far))
    nearer = summed_on_arrival(blocks, near, dim + 1)
    arrived = lax.all_to_all(nearer, far, split_axis=0, concat_axis=0, tiled=True)
    return arrived.sum(axis=0)


def nested_sum(value, axes):
    lines = value.reshape(-1, value.shape[-1])
    padded = rows_for(lines, lax.axis_size(axes[0]) * lax.axis_size(axes[1]))
    whole = gathered_by_axis(summed_rows(padded, axes, 0), axes, 0)
    return lax.slice_in_dim(whole, 0, len(lines)).reshape(value.shape)


def propagate(current, history, pulled, values, columns, start_rows, weight, layer_number):
    feature_width = current.shape[1]
    tile_size = values.shape[2]
    source = jnp.concatenate([current, history, pulled.reshape(-1, feature_width)], axis=0)
    blocks = source.reshape(-1, tile_size, feature_width)
    picked = jnp.take(blocks, columns.reshape(-1), axis=0).reshape(
        columns.shape + (tile_size, feature_width)
    )
    summed = jnp.einsum("btij,btjf->bif", values, picked, preferred_element_type=jnp.float32)
    summed = summed.reshape(current.shape[0], feature_width)
    mixed_rows = (1.0 - restart) * summed + restart * start_rows.astype(jnp.float32)
    mixed_low = mixed_rows.astype(jnp.bfloat16)
    factor = math.log(strength / layer_number + 1.0)
    product = jnp.dot(mixed_low, weight, preferred_element_type=jnp.float32)
    inner_sum = (1.0 - factor) * mixed_rows + factor * product
    return (jnp.maximum(inner_sum, 0.0).astype(jnp.bfloat16), mixed_low)


def local(
    h_zero,
    h_prev,
    hist_a,
    hist_b,
    tile_vals,
    tile_cols,
    pull_rows,
    pull_counts,
    weight_two,
    weight_three,
    grad_out,
):
    wanted = pull_rows[0]
    peer_count, slot_count = wanted.shape
    feature_width = hist_a.shape[1]
    asked_rows = lax.all_to_all(wanted, DEV, split_axis=0, concat_axis=0, tiled=True)
    flat_rows = asked_rows.reshape(-1)
    live_mask = (lax.broadcasted_iota(jnp.int32, wanted.shape, 1) < pull_counts[0][:, None])[
        :, :, None
    ]

    def serve_rows(history):
        return jnp.take(history, flat_rows, axis=0).reshape(peer_count, slot_count, feature_width)

    def trim_rows(arrived):
        return jnp.where(live_mask, arrived, jnp.zeros((), jnp.bfloat16))

    reply_a, reply_b = in_one_piece((serve_rows(hist_a), serve_rows(hist_b)), DEV, 0, 0, 1)
    second, unused_mix = propagate(
        h_prev, hist_a, trim_rows(reply_a), tile_vals, tile_cols, h_zero, weight_two, 2
    )
    fresh_rows = gathered_copies(second, "rep", 0)
    layer_three, mixed_low = propagate(
        second, hist_b, trim_rows(reply_b), tile_vals, tile_cols, h_zero, weight_three, 3
    )
    factor = math.log(strength / 3 + 1.0)
    grad_term = factor * lax.dot_general(
        mixed_low, grad_out, (((0,), (0,)), ((), ())), preferred_element_type=jnp.float32
    )
    grad_total = nested_sum(grad_term, (("dev_0", "dev_1"), ("dev_2", "rep")))
    return (layer_three, fresh_rows, grad_total)


def solution(mesh):
    finer = Mesh(
        mesh.devices.reshape(8, 4, 2, mesh.shape["rep"]), ("dev_0", "dev_1", "dev_2", "rep")
    )
    return jax.shard_map(
        local,
        mesh=finer,
        in_specs=(
            P(DEV_REP, None),
            P(DEV_REP, None),
            P(DEV, None),
            P(DEV, None),
            P(DEV_REP, None, None, None),
            P(DEV_REP, None),
            P(DEV_REP, None, None),
            P(DEV_REP, None),
            P(),
            P(),
            P(DEV_REP, None),
        ),
        out_specs=(P(DEV_REP, None), P(DEV, None), P()),
        check_vma=False,
    )
```

profile of v0, /device:TPU:1, one launch (start us, length us, event | category | flops | bytes accessed | tf_op | source)
XLA Modules:
  0.0 470.5 jit_solution(3735239903999621374)
XLA Ops:
  0.6 22.6 %all_to_all.42 = s32[64,1,128]{2,1,0:T(1,128)S(1)} all-to-all(s32[64,1,128]{2,1,0:T(1,128)} %bitcast.63), channel_id=1, replica_groups=mesh['dev_0'=8,'dev_1'=4,'dev_2'=2,'rep'=4] {'dev_0','dev_1','dev_2'}, dimensions={0} | all-to-all | bytes 65536 | tf_op jit(solution)/shard_map/all_to_all | solution.py:120
  23.3 32.9 %gather_fusion.1 = bf16[8192,256]{1,0:T(8,128)(2,1)} fusion(bf16[4096,256]{1,0:T(8,128)(2,1)} %param.18, s32[8192]{0:T(1024)S(1)} %fusion.12), kind=kCustom, calls=%fused_computation.2.clone | custom fusion | bytes 8421376 | tf_op jit(solution)/shard_map/jit(_take)/gather | solution.py:127
  56.2 33.0 %gather_fusion = bf16[8192,256]{1,0:T(8,128)(2,1)} fusion(bf16[4096,256]{1,0:T(8,128)(2,1)} %param.17, s32[8192]{0:T(1024)S(1)} %fusion.12), kind=kCustom, calls=%fused_computation.clone | custom fusion | bytes 8421376 | tf_op jit(solution)/shard_map/jit(_take)/gather | solution.py:127
  89.1 9.7 %broadcast_select_fusion.3 = (bf16[8192,256]{1,0:T(8,128)(2,1)}, bf16[8192,256]{1,0:T(8,128)(2,1)}) fusion(bf16[8192,256]{1,0:T(8,128)(2,1)} %gather_fusion, pred[8192]{0:T(1024)(128)(4,1)S(1)} %compare_and_fusion, bf16[8192,256]{1,0:T(8,128)(2,1)} %gather_fusion.1), kind=kLoop, calls=%fused_computation.12 | loop fusion | flops 4194304 | bytes 16785408 | tf_op jit(solution)/shard_map/jit(_take)/select_n | solution.py:127
  98.9 7.7 %pad_maximum_fusion = bf16[64,256,256]{2,1,0:T(8,128)(2,1)} fusion(bf16[64,128,256]{2,1,0:T(8,128)(2,1)} %bitcast.57, bf16[64,128,256]{2,1,0:T(8,128)(2,1)} %bitcast.56), kind=kLoop, calls=%fused_computation.4 | loop fusion | flops 16777216 | bytes 16777216 | tf_op jit(solution)/shard_map/concatenate | solution.py:22
  106.6 5.9 %all-to-all-start.1 = ((bf16[64,256,256]{2,1,0:T(8,128)(2,1)}), bf16[64,256,256]{2,1,0:T(8,128)(2,1)}, u32[]{:S(2)}, u32[]{:S(2)}) async-start(bf16[64,256,256]{2,1,0:T(8,128)(2,1)} %pad_maximum_fusion), calls=%async_computation.1 | async-start | bytes 16777216 | tf_op jit(solution)/shard_map/all_to_all | solution.py:25
  112.7 182.9 %all-to-all-done.1 = bf16[64,256,256]{2,1,0:T(8,128)(2,1)} async-done(((bf16[64,256,256]{2,1,0:T(8,128)(2,1)}), bf16[64,256,256]{2,1,0:T(8,128)(2,1)}, u32[]{:S(2)}, u32[]{:S(2)}) %all-to-all-start.1) | async-done | bytes 8388640 | tf_op jit(solution)/shard_map/all_to_all | solution.py:25
  295.7 7.5 %slice_select_fusion.1 = (bf16[64,128,256]{2,1,0:T(8,128)(2,1)S(1)}, bf16[64,128,256]{2,1,0:T(8,128)(2,1)}) fusion(bf16[64,256,256]{2,1,0:T(8,128)(2,1)} %all-to-all-done.1, pred[64,128]{1,0:T(8,128)(4,1)S(1)} %iota_compare_fusion), kind=kLoop, calls=%fused_computation.10 | loop fusion | flops 4194304 | bytes 16785408 | tf_op jit(solution)/shard_map/jit(_where)/select_n | solution.py:130
  303.1 24.0 %pad_maximum_fusion.1 = bf16[13312,256]{1,0:T(8,128)(2,1)} fusion(bf16[8192,256]{1,0:T(8,128)(2,1)S(1)} %bitcast.55, bf16[4096,256]{1,0:T(8,128)(2,1)S(1)} %copy-done.1, bf16[1024,256]{1,0:T(8,128)(2,1)S(1)} %copy-done.9), kind=kLoop, calls=%fused_computation.5 | loop fusion | flops 20447232 | bytes 13631488 | tf_op jit(solution)/shard_map/concatenate | solution.py:89
  327.1 9.0 %gather_fusion.2 = bf16[96,128,256]{2,1,0:T(8,128)(2,1)} fusion(bf16[104,128,256]{2,1,0:T(8,128)(2,1)} %bitcast.53, s32[1024]{0:T(1024)S(1)} %pad_clamp_fusion), kind=kCustom, calls=%fused_computation.1.clone | custom fusion | bytes 12583296 | tf_op jit(solution)/shard_map/jit(_take)/gather | solution.py:91
  336.1 3.4 broadcast_select_fusion
  341.3 1.4 copy-done.3
  342.7 24.0 %pad_maximum_fusion.2 = bf16[13312,256]{1,0:T(8,128)(2,1)} fusion(bf16[8192,256]{1,0:T(8,128)(2,1)S(1)} %bitcast.54, bf16[4096,256]{1,0:T(8,128)(2,1)S(1)} %copy-done.2, bf16[1024,256]{1,0:T(8,128)(2,1)S(1)} %fusion.6), kind=kLoop, calls=%fused_computation.6 | loop fusion | flops 20447232 | bytes 13631488 | tf_op jit(solution)/shard_map/concatenate | solution.py:89
  366.7 9.0 %gather_fusion.3 = bf16[96,128,256]{2,1,0:T(8,128)(2,1)} fusion(bf16[104,128,256]{2,1,0:T(8,128)(2,1)} %bitcast.52, s32[1024]{0:T(1024)S(1)} %pad_clamp_fusion), kind=kCustom, calls=%fused_computation.3.clone | custom fusion | bytes 12583296 | tf_op jit(solution)/shard_map/jit(_take)/gather | solution.py:91
  375.7 3.4 broadcast_select_fusion.1
  381.9 14.4 %all_to_all.43 = f32[8,32,1,256]{3,1,2,0:T(8,128)S(1)} all-to-all(f32[8,32,1,256]{3,1,2,0:T(8,128)S(1)} %bitcast.58), channel_id=1, replica_groups=mesh['dev_0'=8,'dev_1'=4,'dev_2'=2,'rep'=4] {'dev_2','rep'}, dimensions={0} | all-to-all | bytes 524288 | tf_op jit(solution)/shard_map/all_to_all | solution.py:67
  396.4 13.9 %all_to_all.44 = f32[32,1,256]{2,1,0:T(1,128)S(1)} all-to-all(f32[32,1,256]{2,1,0:T(1,128)S(1)} %reduce_sum.21), channel_id=1, replica_groups=mesh['dev_0'=8,'dev_1'=4,'dev_2'=2,'rep'=4] {'dev_0','dev_1'}, dimensions={0} | all-to-all | bytes 65536 | tf_op jit(solution)/shard_map/all_to_all | solution.py:75
  410.4 11.6 %all_to_all.45 = f32[32,1,256]{2,1,0:T(1,128)S(1)} all-to-all(f32[32,1,256]{2,1,0:T(1,128)S(1)} %broadcast_in_dim.47), channel_id=1, replica_groups=mesh['dev_0'=8,'dev_1'=4,'dev_2'=2,'rep'=4] {'dev_0','dev_1'}, dimensions={0} | all-to-all | bytes 65536 | tf_op jit(solution)/shard_map/all_to_all | solution.py:40
  422.0 12.3 %all_to_all.46 = f32[8,32,1,256]{3,1,2,0:T(8,128)S(1)} all-to-all(f32[8,32,1,256]{3,1,2,0:T(8,128)S(1)} %broadcast_in_dim.48), channel_id=1, replica_groups=mesh['dev_0'=8,'dev_1'=4,'dev_2'=2,'rep'=4] {'dev_2','rep'}, dimensions={0} | all-to-all | bytes 524288 | tf_op jit(solution)/shard_map/all_to_all | solution.py:40
  434.4 2.5 broadcast_in_dim.46
  436.9 4.4 all-to-all-start.2
  441.3 2.7 fusion.7
  444.9 22.6 %all-to-all-done.2 = bf16[4,1024,256]{2,1,0:T(8,128)(2,1)} async-done(((bf16[4,1024,256]{2,1,0:T(8,128)(2,1)}), bf16[4,1024,256]{2,1,0:T(8,128)(2,1)}, u32[]{:S(2)}, u32[]{:S(2)}) %all-to-all-start.2) | async-done | bytes 2097184 | tf_op jit(solution)/shard_map/all_to_all | solution.py:40
  467.5 3.0 copy.27
  (48 shorter events, 5.7 us)
Async XLA Ops:
  0.6 338.9 %copy-start = (bf16[8,12,128,128]{3,2,1,0:T(8,128)(2,1)S(1)}, bf16[8,12,128,128]{3,2,1,0:T(8,128)(2,1)}, u32[]{:S(2)}) copy-start(bf16[8,12,128,128]{3,2,1,0:T(8,128)(2,1)} %param.19) | copy-start | bytes 9437188
  106.6 6.0 %copy-start.12 = (s32[8,12]{1,0:T(8,128)S(1)}, s32[8,12]{1,0:T(8,128)}, u32[]{:S(2)}) copy-start(s32[8,12]{1,0:T(8,128)} %param.20) | copy-start | bytes 1156
  106.6 6.1 %copy-start.13 = (s32[1,64]{1,0:T(1,128)S(1)}, s32[1,64]{1,0:T(1,128)}, u32[]{:S(2)}) copy-start(s32[1,64]{1,0:T(1,128)} %param.22) | copy-start | bytes 772
  106.6 189.1 %all-to-all-start.1 = ((bf16[64,256,256]{2,1,0:T(8,128)(2,1)}), bf16[64,256,256]{2,1,0:T(8,128)(2,1)}, u32[]{:S(2)}, u32[]{:S(2)}) async-start(bf16[64,256,256]{2,1,0:T(8,128)(2,1)} %pad_maximum_fusion), calls=%async_computation.1 | async-start | bytes 16777216 | tf_op jit(solution)/shard_map/all_to_all | solution.py:25
  295.6 7.5 %copy-start.1 = (bf16[4096,256]{1,0:T(8,128)(2,1)S(1)}, bf16[4096,256]{1,0:T(8,128)(2,1)}, u32[]{:S(2)}) copy-start(bf16[4096,256]{1,0:T(8,128)(2,1)} %param.17) | copy-start | bytes 6291460
  295.6 7.5 %copy-start.9 = (bf16[1024,256]{1,0:T(8,128)(2,1)S(1)}, bf16[1024,256]{1,0:T(8,128)(2,1)}, u32[]{:S(2)}) copy-start(bf16[1024,256]{1,0:T(8,128)(2,1)} %param.16) | copy-start | bytes 1572868
  339.5 1.3 copy-start.6
  339.5 1.4 copy-start.10
  339.5 1.8 copy-start.2
  339.5 3.2 copy-start.3
  341.3 25.4 %copy-start.5 = (bf16[1024,256]{1,0:T(8,128)(2,1)}, bf16[1024,256]{1,0:T(8,128)(2,1)S(1)}, u32[]{:S(2)}) copy-start(bf16[1024,256]{1,0:T(8,128)(2,1)S(1)} %fusion.6) | copy-start | bytes 1572868
  379.1 1.3 copy-start.7
  379.1 2.4 copy-start.8
  380.5 1.0 copy-start.4
  396.4 44.9 %copy-start.11 = (bf16[256,256]{1,0:T(8,128)(2,1)S(1)}, bf16[256,256]{1,0:T(8,128)(2,1)}, u32[]{:S(2)}) copy-start(bf16[256,256]{1,0:T(8,128)(2,1)} %param.24) | copy-start | bytes 393220
  436.9 30.6 %all-to-all-start.2 = ((bf16[4,1024,256]{2,1,0:T(8,128)(2,1)}), bf16[4,1024,256]{2,1,0:T(8,128)(2,1)}, u32[]{:S(2)}, u32[]{:S(2)}) async-start(bf16[4,1024,256]{2,1,0:T(8,128)(2,1)} %broadcast_in_dim.46), calls=%async_computation.2 | async-start | bytes 4194304 | tf_op jit(solution)/shard_map/all_to_all | solution.py:40
where the time goes:
time: 471 us
  waiting for transfers between devices  206 us (44%)
  local copies, waits for them, and re-layouts  92.9 us (20%)
  other arithmetic  80.1 us (17%)
  blocking collectives  74.9 us (16%)
  starting transfers between devices  10.4 us (2%)
  matrix products  5.81 us (1%)
    all_to_all x1, waiting for transfers between devices, in_one_piece(): lax.all_to_all(both, axis, split_axis=split_dim, concat_axis=concat_dim,...  183 us
    gather x2, local copies, waits for them, and re-layouts, serve_rows(): jnp.take(history, flat_rows, axis=0)  65.9 us
    concatenate x2, other arithmetic, propagate(): jnp.concatenate([current, history, pulled.reshape(-1, feature_width)], ax...  47.9 us
    all_to_all x2, blocking collectives, sent_to_all(): return lax.all_to_all(copies, axis, split_axis=0, concat_axis=0, tiled=True)  23.9 us
    all_to_all x1, waiting for transfers between devices, sent_to_all(): return lax.all_to_all(copies, axis, split_axis=0, concat_axis=0, tiled=True)  22.6 us
    all_to_all x1, blocking collectives, local(): lax.all_to_all(wanted, DEV, split_axis=0, concat_axis=0, tiled=True)  22.6 us
    gather x2, local copies, waits for them, and re-layouts, propagate(): jnp.take(blocks, columns.reshape(-1), axis=0)  17.9 us
    all_to_all x1, blocking collectives, summed_on_arrival(): lax.all_to_all(cut_along(value, dim, length), axis, 0, 0, tiled=True)  14.4 us
  transfers between devices with their start and end apart: 2, of which 2 were waited for; matrix products, arithmetic and copies ran while one was open for 1% of the time, Pallas kernels for 0%

commit v1 on v0

v1 whole, which is shorter than its diff:
```python
import functools
import math

import jax
import jax.numpy as jnp
from jax import lax
from jax.experimental import pallas as pl
from jax.experimental.pallas import tpu as pltpu
from jax.sharding import Mesh
from jax.sharding import PartitionSpec as P

Z, X, C, Y = "dev_0", "dev_1", "dev_2", "rep"
DEV = (Z, X, C)
DEV_REP = (Z, X, C, Y)
MIB = 1024 * 1024

restart = 0.1
strength = 0.5
BF = jnp.bfloat16
F32 = jnp.float32
VMEM = pltpu.VMEM
SMEM = pltpu.SMEM


def vspec():
    return pl.BlockSpec(memory_space=VMEM)


def sspec():
    return pl.BlockSpec(memory_space=SMEM)


def aspec():
    return pl.BlockSpec(memory_space=pl.ANY)


def cost(flops, nbytes):
    return pl.CostEstimate(flops=int(flops), bytes_accessed=int(nbytes), transcendentals=0)


def pack_kernel(inv_ref, cnt_ref, tiles_ref, extra_ref, out_ref, sem):
    groups = out_ref.shape[0]
    for g in range(groups):
        for d in range(4):
            t = inv_ref[g * 4 + d]
            pltpu.make_async_copy(
                tiles_ref.at[t], out_ref.at[g, pl.ds(0, 128), pl.ds(d * 128, 128)], sem.at[g]
            ).start()
    lane = lax.broadcasted_iota(jnp.int32, (128, 128), 1)

    def one(g, carry):
        for d in range(4):
            pltpu.make_async_copy(
                tiles_ref.at[0], out_ref.at[g, pl.ds(0, 128), pl.ds(d * 128, 128)], sem.at[g]
            ).wait()
        for d in range(4):
            here = (pl.ds(0, 128), pl.ds(d * 128, 128))
            tile = out_ref[g, here[0], here[1]].astype(F32)
            tile = jnp.where(lane < cnt_ref[g * 4 + d], tile, 0.0)
            out_ref[g, here[0], here[1]] = tile.astype(BF)
        out_ref[g, 128:144, :] = extra_ref[g]
        return carry

    lax.fori_loop(0, groups, one, 0)


def packed_tiles(inv, cnt, tiles, extra):
    return pl.pallas_call(
        pack_kernel,
        out_shape=jax.ShapeDtypeStruct((16, 144, 512), BF),
        in_specs=[sspec(), sspec(), aspec(), vspec()],
        out_specs=vspec(),
        scratch_shapes=[pltpu.SemaphoreType.DMA((16,))],
        compiler_params=pltpu.CompilerParams(vmem_limit_bytes=16 * MIB),
        cost_estimate=cost(3e9, 5e6),
    )(inv, cnt, tiles, extra)


def pull_kernel(idx_ref, at_ref, v_ref, own_ref, *refs):
    far = refs[:12]
    same_ref, other_ref, stage, table, got, sem = refs[12:]
    turn, core = at_ref[0], at_ref[1]

    def copies(d):
        for q in range(4):
            if d == 0:
                start = pl.multiple_of(lax.rem(turn + q, 4) * 1024, 1024)
                src = own_ref.at[pl.ds(start, 1024), :]
            else:
                src = far[(d - 1) * 4 + q]
            yield pltpu.make_async_copy(src, stage.at[d, pl.ds(q * 1024, 1024), :], sem.at[d])

    for d in range(4):
        for copy in copies(d):
            copy.start()
    for d in range(4):
        for copy in copies(d):
            copy.wait()

        def widen(s, carry):
            r = pl.multiple_of(s * 128, 128)
            rows = stage[d, pl.ds(r, 128), :].astype(F32)
            table[d, pl.ds(2 * r, 128, stride=2), :] = rows[:, :128]
            table[d, pl.ds(2 * r + 1, 128, stride=2), :] = rows[:, 128:]
            return carry

        lax.fori_loop(0, 32, widen, 0)

    def serve(z, which, out):
        g = z * 2 + which
        for d in range(4):
            for j in range(128):
                i = idx_ref[g * 4 + d, j]
                got[pl.ds(2 * (d * 128 + j), 2), :] = table[d, pl.ds(2 * i, 2), :]
        low, high = got[pl.ds(0, 512, stride=2), :], got[pl.ds(1, 512, stride=2), :]
        rows = jnp.concatenate([low, high], axis=1).astype(BF)
        tiles = v_ref[g, 0:128, :]
        flag = v_ref[g, 130:131, :]
        both = jnp.concatenate([tiles * flag, tiles * (1 - flag)], axis=0)
        out[z] = jnp.dot(both, rows, preferred_element_type=F32).astype(out.dtype)

    def one(z, carry):
        serve(z, 1 - core, other_ref)
        return carry

    def two(z, carry):
        serve(z, core, same_ref)
        return carry

    lax.fori_loop(0, 8, one, 0)
    lax.fori_loop(0, 8, two, 0)


def pulled_sums(idx, at, tiles, own, far):
    return pl.pallas_call(
        pull_kernel,
        out_shape=(
            jax.ShapeDtypeStruct((8, 256, 256), F32),
            jax.ShapeDtypeStruct((8, 256, 256), BF),
        ),
        in_specs=[sspec(), sspec(), vspec()] + [aspec()] * 13,
        out_specs=(vspec(), vspec()),
        scratch_shapes=[
            VMEM((4, 4096, 256), BF),
            VMEM((4, 8192, 128), F32),
            VMEM((1024, 128), F32),
            pltpu.SemaphoreType.DMA((4,)),
        ],
        compiler_params=pltpu.CompilerParams(vmem_limit_bytes=48 * MIB),
        cost_estimate=cost(20e9, 20e6),
    )(idx, at, tiles, own, *far)


def home_kernel(first, cols_ref, tiles_ref, cur_ref, hist_ref, out_ref):
    for i in range(8):
        total = None
        for t in range(first, 4):
            b = cols_ref[i, t]
            if t == 0:
                block = cur_ref[pl.ds(pl.multiple_of(b * 128, 128), 128), :]
            else:
                block = hist_ref[pl.ds(pl.multiple_of((b - 8) * 128, 128), 128), :]
            part = jnp.dot(tiles_ref[i, t], block, preferred_element_type=F32)
            total = part if total is None else total + part
        out_ref[i] = total


def home_sums(first, cols, tiles, cur, hist):
    return pl.pallas_call(
        functools.partial(home_kernel, first),
        grid=(1,),
        out_shape=jax.ShapeDtypeStruct((8, 128, 256), F32),
        in_specs=[
            sspec(),
            pl.BlockSpec((8, 4, 128, 128), lambda i: (0, 0, 0, 0)),
            pl.BlockSpec((1024, 256), lambda i: (0, 0)),
            pl.BlockSpec((4096, 256), lambda i: (0, 0)),
        ],
        out_specs=pl.BlockSpec((8, 128, 256), lambda i: (0, 0, 0)),
        compiler_params=pltpu.CompilerParams(vmem_limit_bytes=24 * MIB),
        cost_estimate=cost(3e9, 5e6),
    )(cols, tiles, cur, hist)


def gathered(total, at_ref, arrived_ref):
    for k in range(8):
        for s in range(2):
            i = at_ref[k, s]
            total[i] = total[i] + arrived_ref[k, pl.ds(s * 128, 128), :].astype(F32)


def layer_two_kernel(at_ref, home_ref, arrived_ref, zero_ref, weight_ref, out_ref, total):
    total[...] = home_ref[...]
    gathered(total, at_ref, arrived_ref)
    factor = math.log(strength / 2 + 1.0)
    mixed = (1.0 - restart) * total[...].reshape(1024, 256) + restart * zero_ref[...].astype(F32)
    product = jnp.dot(mixed.astype(BF), weight_ref[...], preferred_element_type=F32)
    out_ref[...] = jnp.maximum((1.0 - factor) * mixed + factor * product, 0.0).astype(BF)


def layer_two(at, home, arrived, zero, weight):
    return pl.pallas_call(
        layer_two_kernel,
        out_shape=jax.ShapeDtypeStruct((1024, 256), BF),
        in_specs=[sspec()] + [vspec()] * 4,
        out_specs=vspec(),
        scratch_shapes=[VMEM((8, 128, 256), F32)],
        compiler_params=pltpu.CompilerParams(vmem_limit_bytes=24 * MIB),
        cost_estimate=cost(1e9, 4e6),
    )(at, home, arrived, zero, weight)


def layer_three_kernel(
    at_ref, cols_ref, home_ref, arrived_ref, tiles_ref, cur_ref, zero_ref, weight_ref, grad_ref,
    out_ref, term_ref, total,
):
    for i in range(8):
        block = cur_ref[pl.ds(pl.multiple_of(cols_ref[i, 0] * 128, 128), 128), :]
        total[i] = home_ref[i] + jnp.dot(tiles_ref[i, 0], block, preferred_element_type=F32)
    gathered(total, at_ref, arrived_ref)
    factor = math.log(strength / 3 + 1.0)
    mixed = (1.0 - restart) * total[...].reshape(1024, 256) + restart * zero_ref[...].astype(F32)
    low = mixed.astype(BF)
    product = jnp.dot(low, weight_ref[...], preferred_element_type=F32)
    out_ref[...] = jnp.maximum((1.0 - factor) * mixed + factor * product, 0.0).astype(BF)
    term_ref[...] = factor * lax.dot_general(
        low, grad_ref[...], (((0,), (0,)), ((), ())), preferred_element_type=F32
    )


def layer_three_call(at, cols, home, arrived, tiles, cur, zero, weight, grad):
    whole = lambda *shape: pl.BlockSpec(shape, lambda i: (0,) * len(shape))
    return pl.pallas_call(
        layer_three_kernel,
        grid=(1,),
        out_shape=(
            jax.ShapeDtypeStruct((1024, 256), BF),
            jax.ShapeDtypeStruct((256, 256), F32),
        ),
        in_specs=[
            sspec(), sspec(), whole(8, 128, 256), whole(8, 256, 256), whole(8, 1, 128, 128),
            whole(1024, 256), whole(1024, 256), whole(256, 256), whole(1024, 256),
        ],
        out_specs=(whole(1024, 256), whole(256, 256)),
        scratch_shapes=[VMEM((8, 128, 256), F32)],
        compiler_params=pltpu.CompilerParams(vmem_limit_bytes=32 * MIB),
        cost_estimate=cost(1e9, 4e6),
    )(at, cols, home, arrived, tiles, cur, zero, weight, grad)


def in_order(blocks, dim):
    shape = list(blocks.shape[1:])
    shape[dim] *= blocks.shape[0]
    return jnp.moveaxis(blocks, 0, dim).reshape(shape)


def sent_to_all(value, axis):
    copies = jnp.broadcast_to(value, (lax.axis_size(axis), *value.shape))
    return lax.all_to_all(copies, axis, split_axis=0, concat_axis=0, tiled=True)


def gathered_by_axis(value, axes, dim):
    far, near = axes
    initial = sent_to_all(value, far)
    blocks = jnp.swapaxes(sent_to_all(initial, near), 0, 1)
    return in_order(blocks.reshape(-1, *value.shape), dim)


def cut_along(value, dim, length):
    shape = value.shape
    blocks = value.reshape(*shape[:dim], length, shape[dim] // length, *shape[dim + 1 :])
    return jnp.moveaxis(blocks, dim, 0)


def summed_on_arrival(value, axis, dim):
    length = lax.axis_size(axis)
    blocks = lax.all_to_all(cut_along(value, dim, length), axis, 0, 0, tiled=True)
    return jnp.sum(blocks, axis=0)


def summed_rows(value, axes, dim):
    far, near = axes
    blocks = cut_along(value, dim, lax.axis_size(far))
    nearer = summed_on_arrival(blocks, near, dim + 1)
    arrived = lax.all_to_all(nearer, far, split_axis=0, concat_axis=0, tiled=True)
    return arrived.sum(axis=0)


def nested_sum(value, axes):
    return gathered_by_axis(summed_rows(value, axes, 0), axes, 0)


def shifted(value, axis, by):
    n = lax.axis_size(axis)
    return lax.ppermute(value, axis, [((i + by) % n, i) for i in range(n)])


def local(
    h_zero, h_prev, hist_a, hist_b, tile_vals, tile_cols, pull_rows, pull_counts,
    weight_two, weight_three, grad_out,
):
    x, core, turn = lax.axis_index(X), lax.axis_index(C), lax.axis_index(Y)

    def shard(history):
        quarters = history.reshape(4, 1024, 256)
        mine = [
            lax.dynamic_index_in_dim(quarters, lax.rem(turn + q, 4), 0, keepdims=False)
            for q in range(2)
        ]
        far = []
        for d in (1, 3, 2):
            a, b = [shifted(m, X, d) for m in mine]
            far.append((d, [a, b, shifted(b, Y, 1), shifted(a, Y, 3)]))
        return [piece for _, pieces in sorted(far, key=lambda f: f[0]) for piece in pieces]

    far_a = shard(hist_a)
    k = lax.broadcasted_iota(jnp.int32, (8, 2, 4), 0)
    c = lax.broadcasted_iota(jnp.int32, (8, 2, 4), 1)
    d = lax.broadcasted_iota(jnp.int32, (8, 2, 4), 2)
    owner = (8 * k + 2 * lax.rem(x + d, 4) + c).reshape(64)
    named = tile_cols[:, 4:].reshape(64) - 40
    block = lax.broadcasted_iota(jnp.int32, (8, 8), 0).reshape(64)
    place = (lax.broadcasted_iota(jnp.int32, (8, 8), 1) + 12 * block.reshape(8, 8) + 4).reshape(64)
    is_it = named[None, :] == jnp.arange(64, dtype=jnp.int32)[:, None]
    tile_of = jnp.sum(jnp.where(is_it, place[None, :], 0), axis=1)
    block_of = jnp.sum(jnp.where(is_it, block[None, :], 0), axis=1).reshape(8, 8)
    ends = jnp.stack([block_of[:, 0], block_of[:, 7]], axis=1)
    first = (block_of == ends[:, :1]).reshape(64)
    inv = jnp.take(tile_of, owner)
    cnt = jnp.take(pull_counts[0], owner)
    rows = lax.rem(jnp.take(pull_rows[0], owner, axis=0) + (4096 - 1024 * turn), 4096)
    flag = jnp.broadcast_to(jnp.take(first, owner)[:, None], (64, 128))
    extra = jnp.stack([rows // 64, lax.rem(rows, 64), flag.astype(jnp.int32)], axis=1)
    extra = extra.reshape(16, 4, 3, 128).transpose(0, 2, 1, 3).reshape(16, 3, 512)
    extra = jnp.pad(extra.astype(BF), ((0, 0), (0, 13), (0, 0)))
    tiles = packed_tiles(inv, cnt, tile_vals.reshape(96, 128, 128), extra)
    tiles = lax.all_to_all(tiles, (Z, C), split_axis=0, concat_axis=0, tiled=True)
    digits = tiles[:, 128:130, :].astype(F32).astype(jnp.int32)
    idx = (digits[:, 0] * 64 + digits[:, 1]).reshape(64, 128)
    at = jnp.stack([turn, core])

    far_b = shard(hist_b)
    home_a = home_sums(0, tile_cols, tile_vals, h_prev, hist_a)
    home_b = home_sums(1, tile_cols, tile_vals, h_prev, hist_b)

    def arrived_sums(history, far):
        same, other = pulled_sums(idx, at, tiles, history, far)
        out = (same + shifted(other, C, 1).astype(F32)).astype(BF)
        return lax.all_to_all(out, Z, split_axis=0, concat_axis=0, tiled=True)

    arrived_a = arrived_sums(hist_a, far_a)
    second = layer_two(ends, home_a, arrived_a, h_zero, weight_two)
    fresh_rows = in_order(sent_to_all(second, Y), 0)
    arrived_b = arrived_sums(hist_b, far_b)
    layer_three, term = layer_three_call(
        ends, tile_cols, home_b, arrived_b, tile_vals, second, h_zero, weight_three, grad_out
    )
    grad_total = nested_sum(term, ((Z, X), (C, Y)))
    return (layer_three, fresh_rows, grad_total)


def solution(mesh):
    finer = Mesh(mesh.devices.reshape(8, 4, 2, mesh.shape["rep"]), (Z, X, C, Y))
    return jax.shard_map(
        local,
        mesh=finer,
        in_specs=(
            P(DEV_REP, None),
            P(DEV_REP, None),
            P(DEV, None),
            P(DEV, None),
            P(DEV_REP, None, None, None),
            P(DEV_REP, None),
            P(DEV_REP, None, None),
            P(DEV_REP, None),
            P(),
            P(),
            P(DEV_REP, None),
        ),
        out_specs=(P(DEV_REP, None), P(DEV, None), P()),
        check_vma=False,
    )
```

time: 471 us -> 359 us (0.76)
  other arithmetic: 80.1 us -> 8.36 us
  local copies, waits for them, and re-layouts: 92.9 us -> 29.9 us
  starting transfers between devices: 10.4 us -> 63.3 us
  Pallas kernels: 0 us -> 46.8 us
  waiting for transfers between devices: 206 us -> 162 us
  blocking collectives: 74.9 us -> 46.9 us
  matrix products: 5.81 us -> 0 us
    all_to_all x1 -> x3, waiting for transfers between devices: 183 us -> 20.7 us  [the longest x2 20.7 us: arrived_sums(): return lax.all_to_all(out, Z, split_axis=0, concat_axis=0, tiled=True)]
    ppermute x0 -> x26, waiting for transfers between devices: none -> 116 us  [shifted(): return lax.ppermute(value, axis, [((i + by) % n, i) for i in range(n)])]
    gather x4 -> x5, local copies, waits for them, and re-layouts: 83.8 us -> 3.04 us  [the longest x2 0.88 us: local(): flag = jnp.broadcast_to(jnp.take(first, owner)[:, None], (64, 128))]
    concatenate x3 -> x0, other arithmetic: 55.6 us -> none  [the longest x2 47.9 us: propagate(): jnp.concatenate([current, history, pulled.reshape(-1, feature_width)], ax...]
    pallas_call x0 -> x7, Pallas kernels: none -> 46.8 us  [the longest x2 37.4 us: pulled_sums(): pl.pallas_call(pull_kernel, out_shape=(jax.ShapeDtypeStruct((8, 256, 256)...]
    ppermute x0 -> x26, starting transfers between devices: none -> 36.7 us  [shifted(): return lax.ppermute(value, axis, [((i + by) % n, i) for i in range(n)])]
    select_n x5 -> x3, other arithmetic: 24.1 us -> 0.03 us  [the longest x1 0.01 us: local(): jnp.take(pull_rows[0], owner, axis=0) + (4096 - 1024 * turn)]
    all_to_all x1 -> x0, blocking collectives: 22.6 us -> none  [local(): lax.all_to_all(wanted, DEV, split_axis=0, concat_axis=0, tiled=True)]
  transfers between devices with their start and end apart: 2 -> 30, of which waited for: 2 -> 14; matrix products, arithmetic and copies ran while one was open for 1% -> 3% of each run, Pallas kernels for 0% -> 11%
where the time goes in v1:
time: 359 us; the launch traced here: 358 us
  waiting for transfers between devices  162 us (45%)
  starting transfers between devices  63.3 us (18%)
  blocking collectives  46.9 us (13%)
  Pallas kernels  46.8 us (13%)
  local copies, waits for them, and re-layouts  29.9 us (8%)
  other arithmetic  8.36 us (2%)
    ppermute x26, waiting for transfers between devices, shifted(): return lax.ppermute(value, axis, [((i + by) % n, i) for i in range(n)])  116 us
    pallas_call x2, Pallas kernels, pulled_sums(): pl.pallas_call(pull_kernel, out_shape=(jax.ShapeDtypeStruct((8, 256, 256)...  37.4 us
    ppermute x26, starting transfers between devices, shifted(): return lax.ppermute(value, axis, [((i + by) % n, i) for i in range(n)])  36.7 us
    all_to_all x1, waiting for transfers between devices, sent_to_all(): return lax.all_to_all(copies, axis, split_axis=0, concat_axis=0, tiled=True)  25.2 us
    all_to_all x2, blocking collectives, sent_to_all(): return lax.all_to_all(copies, axis, split_axis=0, concat_axis=0, tiled=True)  23.9 us
    all_to_all x2, waiting for transfers between devices, arrived_sums(): return lax.all_to_all(out, Z, split_axis=0, concat_axis=0, tiled=True)  20.7 us
    unnamed x54, local copies, waits for them, and re-layouts  19.5 us
    all_to_all x1, blocking collectives, summed_rows(): lax.all_to_all(nearer, far, split_axis=0, concat_axis=0, tiled=True)  13.6 us
  transfers between devices with their start and end apart: 30, of which 14 were waited for; matrix products, arithmetic and copies ran while one was open for 3% of the time, Pallas kernels for 11%

profile of v1, /device:TPU:1, one launch (start us, length us, event | category | flops | bytes accessed | tf_op | source)
XLA Modules:
  0.0 358.3 jit_solution(1686502911116040369)
XLA Ops:
  8.6 3.4 shard_map.131
  12.0 10.1 %all-to-all-start = ((bf16[16,144,512]{2,1,0:T(8,128)(2,1)}), bf16[16,144,512]{2,1,0:T(8,128)(2,1)}, u32[]{:S(2)}, u32[]{:S(2)}) async-start(bf16[16,144,512]{2,1,0:T(8,128)(2,1)} %shard_map.131), calls=%async_computation | async-start | bytes 4718592 | tf_op jit(solution)/shard_map/all_to_all | solution.py:337
  30.1 7.0 %collective-permute-done.14.refs_1_ = bf16[1024,256]{1,0:T(8,128)(2,1)S(1)} collective-permute-done((bf16[1024,256]{1,0:T(8,128)(2,1)}, bf16[1024,256]{1,0:T(8,128)(2,1)S(1)}, u32[]{:S(2)}, u32[]{:S(2)}) %collective-permute-start.14) | collective-permute-done | bytes 524320 | tf_op jit(solution)/shard_map/ppermute | solution.py:295
  38.1 32.6 %collective-permute-done.13.refs_0_ = bf16[1024,256]{1,0:T(8,128)(2,1)S(1)} collective-permute-done((bf16[1024,256]{1,0:T(8,128)(2,1)}, bf16[1024,256]{1,0:T(8,128)(2,1)S(1)}, u32[]{:S(2)}, u32[]{:S(2)}) %collective-permute-start.13) | collective-permute-done | bytes 524320 | tf_op jit(solution)/shard_map/ppermute | solution.py:295
  89.7 5.1 %collective-permute-done.19.refs_6_ = bf16[1024,256]{1,0:T(8,128)(2,1)} collective-permute-done((bf16[1024,256]{1,0:T(8,128)(2,1)S(1)}, bf16[1024,256]{1,0:T(8,128)(2,1)}, u32[]{:S(2)}, u32[]{:S(2)}) %collective-permute-start.19) | collective-permute-done | bytes 524320 | tf_op jit(solution)/shard_map/ppermute | solution.py:295
  94.8 3.8 %collective-permute-start.1 = (bf16[1024,256]{1,0:T(8,128)(2,1)}, bf16[1024,256]{1,0:T(8,128)(2,1)S(1)}, u32[]{:S(2)}, u32[]{:S(2)}) collective-permute-start(bf16[1024,256]{1,0:T(8,128)(2,1)} %get-tuple-element.22), channel_id=1, source_target_pairs={{8,0},{16,8},{24,16},{0,24},{9,1},{17,9},{25,17},{1,25},{10,2},{18... | collective-permute-start | bytes 1572872 | tf_op jit(solution)/shard_map/ppermute | solution.py:295
  100.2 5.9 %collective-permute-done.23.refs_10_ = bf16[1024,256]{1,0:T(8,128)(2,1)} collective-permute-done((bf16[1024,256]{1,0:T(8,128)(2,1)}, bf16[1024,256]{1,0:T(8,128)(2,1)}, u32[]{:S(2)}, u32[]{:S(2)}) %collective-permute-start.23) | collective-permute-done | bytes 524320 | tf_op jit(solution)/shard_map/ppermute | solution.py:295
  106.1 5.4 %collective-permute-done.24.refs_11_ = bf16[1024,256]{1,0:T(8,128)(2,1)} collective-permute-done((bf16[1024,256]{1,0:T(8,128)(2,1)}, bf16[1024,256]{1,0:T(8,128)(2,1)}, u32[]{:S(2)}, u32[]{:S(2)}) %collective-permute-start.24) | collective-permute-done | bytes 524320 | tf_op jit(solution)/shard_map/ppermute | solution.py:295
  114.6 18.6 %shard_map.134 = (f32[8,256,256]{2,1,0:T(8,128)}, bf16[8,256,256]{2,1,0:T(8,128)(2,1)}) custom-call(s32[64,128]{1,0:T(8,128)S(1)} %bitcast.42, s32[2]{0:T(128)S(1)} %pad_add_fusion.1.at_ref, bf16[16,144,512]{2,1,0:T(8,128)(2,1)} %all-to-all-done.v_ref, bf16[4096,256]{1,0:T(8,128)(2,1)} %own_ref.3, bf16[1024,256]{1,0:T(8,128)(2,1)S(1)} %collective-permute-done.13.refs_0_, ...), custom_call_target="tpu_custom_call" | custom-call | flops 20000000000 | bytes 20000000 | tf_op jit(solution)/shard_map/pallas_call | solution.py:135
  135.6 3.6 collective-permute-start
  139.2 3.0 collective-permute-start.4
  142.2 30.7 %collective-permute-done.refs_0_ = bf16[1024,256]{1,0:T(8,128)(2,1)S(1)} collective-permute-done((bf16[1024,256]{1,0:T(8,128)(2,1)S(1)}, bf16[1024,256]{1,0:T(8,128)(2,1)S(1)}, u32[]{:S(2)}, u32[]{:S(2)}) %collective-permute-start) | collective-permute-done | bytes 524320 | tf_op jit(solution)/shard_map/ppermute | solution.py:295
  181.9 6.4 %all-to-all-start.2 = ((bf16[8,256,256]{2,1,0:T(8,128)(2,1)}), bf16[8,256,256]{2,1,0:T(8,128)(2,1)S(1)}, u32[]{:S(2)}, u32[]{:S(2)}) async-start(bf16[8,256,256]{2,1,0:T(8,128)(2,1)} %add_convert_fusion), calls=%async_computation.2 | async-start | bytes 2097152 | tf_op jit(solution)/shard_map/all_to_all | solution.py:349
  188.3 9.6 %collective-permute-done.3.refs_3_ = bf16[1024,256]{1,0:T(8,128)(2,1)} collective-permute-done((bf16[1024,256]{1,0:T(8,128)(2,1)S(1)}, bf16[1024,256]{1,0:T(8,128)(2,1)}, u32[]{:S(2)}, u32[]{:S(2)}) %collective-permute-start.3) | collective-permute-done | bytes 524320 | tf_op jit(solution)/shard_map/ppermute | solution.py:295
  197.9 11.2 %collective-permute-done.7.refs_7_ = bf16[1024,256]{1,0:T(8,128)(2,1)} collective-permute-done((bf16[1024,256]{1,0:T(8,128)(2,1)}, bf16[1024,256]{1,0:T(8,128)(2,1)}, u32[]{:S(2)}, u32[]{:S(2)}) %collective-permute-start.7) | collective-permute-done | bytes 524320 | tf_op jit(solution)/shard_map/ppermute | solution.py:295
  210.2 18.8 %shard_map.132 = (f32[8,256,256]{2,1,0:T(8,128)}, bf16[8,256,256]{2,1,0:T(8,128)(2,1)}) custom-call(s32[64,128]{1,0:T(8,128)S(1)} %bitcast.43, s32[2]{0:T(128)S(1)} %pad_add_fusion.1.at_ref, bf16[16,144,512]{2,1,0:T(8,128)(2,1)} %all-to-all-done.v_ref, bf16[4096,256]{1,0:T(8,128)(2,1)} %own_ref.2, bf16[1024,256]{1,0:T(8,128)(2,1)S(1)} %collective-permute-done.refs_0_, ...), custom_call_target="tpu_custom_call" | custom-call | flops 20000000000 | bytes 20000000 | tf_op jit(solution)/shard_map/pallas_call | solution.py:135
  236.3 6.5 %all-to-all-start.1 = ((bf16[8,256,256]{2,1,0:T(8,128)(2,1)}), bf16[8,256,256]{2,1,0:T(8,128)(2,1)S(1)}, u32[]{:S(2)}, u32[]{:S(2)}) async-start(bf16[8,256,256]{2,1,0:T(8,128)(2,1)} %add_convert_fusion.1), calls=%async_computation.1 | async-start | bytes 2097152 | tf_op jit(solution)/shard_map/all_to_all | solution.py:349
  251.4 20.7 %all-to-all-done.1.arrived_ref = bf16[8,256,256]{2,1,0:T(8,128)(2,1)S(1)} async-done(((bf16[8,256,256]{2,1,0:T(8,128)(2,1)}), bf16[8,256,256]{2,1,0:T(8,128)(2,1)S(1)}, u32[]{:S(2)}, u32[]{:S(2)}) %all-to-all-start.1) | async-done | bytes 1048608 | tf_op jit(solution)/shard_map/all_to_all | solution.py:349
  278.7 9.4 %all_to_all.43 = f32[8,32,1,256]{3,1,2,0:T(8,128)S(1)} all-to-all(f32[8,32,1,256]{3,1,2,0:T(8,128)S(1)} %bitcast.46), channel_id=1, replica_groups=mesh['dev_0'=8,'dev_1'=4,'dev_2'=2,'rep'=4] {'dev_2','rep'}, dimensions={0} | all-to-all | bytes 524288 | tf_op jit(solution)/shard_map/all_to_all | solution.py:277
  288.2 13.6 %all_to_all.44 = f32[32,1,256]{2,1,0:T(1,128)S(1)} all-to-all(f32[32,1,256]{2,1,0:T(1,128)S(1)} %reduce_sum.41), channel_id=1, replica_groups=mesh['dev_0'=8,'dev_1'=4,'dev_2'=2,'rep'=4] {'dev_0','dev_1'}, dimensions={0} | all-to-all | bytes 65536 | tf_op jit(solution)/shard_map/all_to_all | solution.py:285
  301.9 11.6 %all_to_all.45 = f32[32,1,256]{2,1,0:T(1,128)S(1)} all-to-all(f32[32,1,256]{2,1,0:T(1,128)S(1)} %broadcast_in_dim.65), channel_id=1, replica_groups=mesh['dev_0'=8,'dev_1'=4,'dev_2'=2,'rep'=4] {'dev_0','dev_1'}, dimensions={0} | all-to-all | bytes 65536 | tf_op jit(solution)/shard_map/all_to_all | solution.py:259
  313.5 12.3 %all_to_all.46 = f32[8,32,1,256]{3,1,2,0:T(8,128)S(1)} all-to-all(f32[8,32,1,256]{3,1,2,0:T(8,128)S(1)} %broadcast_in_dim.66), channel_id=1, replica_groups=mesh['dev_0'=8,'dev_1'=4,'dev_2'=2,'rep'=4] {'dev_2','rep'}, dimensions={0} | all-to-all | bytes 524288 | tf_op jit(solution)/shard_map/all_to_all | solution.py:259
  327.3 3.6 %all-to-all-start.3 = ((bf16[4,1024,256]{2,1,0:T(8,128)(2,1)}), bf16[4,1024,256]{2,1,0:T(8,128)(2,1)S(1)}, u32[]{:S(2)}, u32[]{:S(2)}) async-start(bf16[4,1024,256]{2,1,0:T(8,128)(2,1)} %broadcast_in_dim.64), calls=%async_computation.3 | async-start | bytes 4194304 | tf_op jit(solution)/shard_map/all_to_all | solution.py:259
  331.8 25.2 %all-to-all-done.3 = bf16[4,1024,256]{2,1,0:T(8,128)(2,1)S(1)} async-done(((bf16[4,1024,256]{2,1,0:T(8,128)(2,1)}), bf16[4,1024,256]{2,1,0:T(8,128)(2,1)S(1)}, u32[]{:S(2)}, u32[]{:S(2)}) %all-to-all-start.3) | async-done | bytes 2097184 | tf_op jit(solution)/shard_map/all_to_all | solution.py:259
  (163 shorter events, 79.4 us)
Async XLA Ops:
  12.0 73.1 %all-to-all-start = ((bf16[16,144,512]{2,1,0:T(8,128)(2,1)}), bf16[16,144,512]{2,1,0:T(8,128)(2,1)}, u32[]{:S(2)}, u32[]{:S(2)}) async-start(bf16[16,144,512]{2,1,0:T(8,128)(2,1)} %shard_map.131), calls=%async_computation | async-start | bytes 4718592 | tf_op jit(solution)/shard_map/all_to_all | solution.py:337
  25.7 45.0 %collective-permute-start.13 = (bf16[1024,256]{1,0:T(8,128)(2,1)}, bf16[1024,256]{1,0:T(8,128)(2,1)S(1)}, u32[]{:S(2)}, u32[]{:S(2)}) collective-permute-start(bf16[1024,256]{1,0:T(8,128)(2,1)} %get-tuple-element.21), channel_id=1, source_target_pairs={{8,0},{16,8},{24,16},{0,24},{9,1},{17,9},{25,17},{1,25},{10,2},{18... | collective-permute-start | bytes 1572872 | tf_op jit(solution)/shard_map/ppermute | solution.py:295
  26.3 49.4 %collective-permute-start.18 = (bf16[1024,256]{1,0:T(8,128)(2,1)}, bf16[1024,256]{1,0:T(8,128)(2,1)S(1)}, u32[]{:S(2)}, u32[]{:S(2)}) collective-permute-start(bf16[1024,256]{1,0:T(8,128)(2,1)} %get-tuple-element.20), channel_id=1, source_target_pairs={{16,0},{24,8},{0,16},{8,24},{17,1},{25,9},{1,17},{9,25},{18,2},{26... | collective-permute-start | bytes 1572872 | tf_op jit(solution)/shard_map/ppermute | solution.py:295
  26.5 49.2 %collective-permute-start.17 = (bf16[1024,256]{1,0:T(8,128)(2,1)}, bf16[1024,256]{1,0:T(8,128)(2,1)S(1)}, u32[]{:S(2)}, u32[]{:S(2)}) collective-permute-start(bf16[1024,256]{1,0:T(8,128)(2,1)} %get-tuple-element.21), channel_id=1, source_target_pairs={{16,0},{24,8},{0,16},{8,24},{17,1},{25,9},{1,17},{9,25},{18,2},{26... | collective-permute-start | bytes 1572872 | tf_op jit(solution)/shard_map/ppermute | solution.py:295
  29.2 49.1 %collective-permute-start.22 = (bf16[1024,256]{1,0:T(8,128)(2,1)}, bf16[1024,256]{1,0:T(8,128)(2,1)}, u32[]{:S(2)}, u32[]{:S(2)}) collective-permute-start(bf16[1024,256]{1,0:T(8,128)(2,1)} %get-tuple-element.20), channel_id=1, source_target_pairs={{24,0},{0,8},{8,16},{16,24},{25,1},{1,9},{9,17},{17,25},{26,2},{2,... | collective-permute-start | bytes 1572872 | tf_op jit(solution)/shard_map/ppermute | solution.py:295
  37.1 42.0 %collective-permute-start.21 = (bf16[1024,256]{1,0:T(8,128)(2,1)}, bf16[1024,256]{1,0:T(8,128)(2,1)}, u32[]{:S(2)}, u32[]{:S(2)}) collective-permute-start(bf16[1024,256]{1,0:T(8,128)(2,1)} %get-tuple-element.21), channel_id=1, source_target_pairs={{24,0},{0,8},{8,16},{16,24},{25,1},{1,9},{9,17},{17,25},{26,2},{2,... | collective-permute-start | bytes 1572872 | tf_op jit(solution)/shard_map/ppermute | solution.py:295
  75.7 19.1 %collective-permute-start.19 = (bf16[1024,256]{1,0:T(8,128)(2,1)S(1)}, bf16[1024,256]{1,0:T(8,128)(2,1)}, u32[]{:S(2)}, u32[]{:S(2)}) collective-permute-start(bf16[1024,256]{1,0:T(8,128)(2,1)S(1)} %collective-permute-done.18.refs_5_), channel_id=1, source_target_pairs={{1,0},{2,1},{3,2},{0,3},{5,4},{6,5},{7,6},{4,7},{9,8},{10,9},{11,1... | collective-permute-start | bytes 1572872 | tf_op jit(solution)/shard_map/ppermute | solution.py:295
  78.4 21.9 %collective-permute-start.20 = (bf16[1024,256]{1,0:T(8,128)(2,1)S(1)}, bf16[1024,256]{1,0:T(8,128)(2,1)}, u32[]{:S(2)}, u32[]{:S(2)}) collective-permute-start(bf16[1024,256]{1,0:T(8,128)(2,1)S(1)} %collective-permute-done.17.refs_4_), channel_id=1, source_target_pairs={{3,0},{0,1},{1,2},{2,3},{7,4},{4,5},{5,6},{6,7},{11,8},{8,9},{9,10... | collective-permute-start | bytes 1572872 | tf_op jit(solution)/shard_map/ppermute | solution.py:295
  79.2 26.9 %collective-permute-start.23 = (bf16[1024,256]{1,0:T(8,128)(2,1)}, bf16[1024,256]{1,0:T(8,128)(2,1)}, u32[]{:S(2)}, u32[]{:S(2)}) collective-permute-start(bf16[1024,256]{1,0:T(8,128)(2,1)} %collective-permute-done.22.refs_9_), channel_id=1, source_target_pairs={{1,0},{2,1},{3,2},{0,3},{5,4},{6,5},{7,6},{4,7},{9,8},{10,9},{11,1... | collective-permute-start | bytes 1572872 | tf_op jit(solution)/shard_map/ppermute | solution.py:295
  84.3 27.2 %collective-permute-start.24 = (bf16[1024,256]{1,0:T(8,128)(2,1)}, bf16[1024,256]{1,0:T(8,128)(2,1)}, u32[]{:S(2)}, u32[]{:S(2)}) collective-permute-start(bf16[1024,256]{1,0:T(8,128)(2,1)} %collective-permute-done.21.refs_8_), channel_id=1, source_target_pairs={{3,0},{0,1},{1,2},{2,3},{7,4},{4,5},{5,6},{6,7},{11,8},{8,9},{9,10... | collective-permute-start | bytes 1572872 | tf_op jit(solution)/shard_map/ppermute | solution.py:295
  89.7 49.5 %collective-permute-start.9 = (bf16[1024,256]{1,0:T(8,128)(2,1)}, bf16[1024,256]{1,0:T(8,128)(2,1)S(1)}, u32[]{:S(2)}, u32[]{:S(2)}) collective-permute-start(bf16[1024,256]{1,0:T(8,128)(2,1)} %get-tuple-element.22), channel_id=1, source_target_pairs={{24,0},{0,8},{8,16},{16,24},{25,1},{1,9},{9,17},{17,25},{26,2},{2,... | collective-permute-start | bytes 1572872 | tf_op jit(solution)/shard_map/ppermute | solution.py:295
  94.8 47.4 %collective-permute-start.1 = (bf16[1024,256]{1,0:T(8,128)(2,1)}, bf16[1024,256]{1,0:T(8,128)(2,1)S(1)}, u32[]{:S(2)}, u32[]{:S(2)}) collective-permute-start(bf16[1024,256]{1,0:T(8,128)(2,1)} %get-tuple-element.22), channel_id=1, source_target_pairs={{8,0},{16,8},{24,16},{0,24},{9,1},{17,9},{25,17},{1,25},{10,2},{18... | collective-permute-start | bytes 1572872 | tf_op jit(solution)/shard_map/ppermute | solution.py:295
  100.2 39.0 %collective-permute-start.8 = (bf16[1024,256]{1,0:T(8,128)(2,1)}, bf16[1024,256]{1,0:T(8,128)(2,1)S(1)}, u32[]{:S(2)}, u32[]{:S(2)}) collective-permute-start(bf16[1024,256]{1,0:T(8,128)(2,1)} %get-tuple-element.23), channel_id=1, source_target_pairs={{24,0},{0,8},{8,16},{16,24},{25,1},{1,9},{9,17},{17,25},{26,2},{2,... | collective-permute-start | bytes 1572872 | tf_op jit(solution)/shard_map/ppermute | solution.py:295
  133.2 45.8 %collective-permute-start.25 = (bf16[8,256,256]{2,1,0:T(8,128)(2,1)}, bf16[8,256,256]{2,1,0:T(8,128)(2,1)S(1)}, u32[]{:S(2)}, u32[]{:S(2)}) collective-permute-start(bf16[8,256,256]{2,1,0:T(8,128)(2,1)} %get-tuple-element.13), channel_id=1, source_target_pairs={{4,0},{0,4},{5,1},{1,5},{6,2},{2,6},{7,3},{3,7},{12,8},{8,12},{13,... | collective-permute-start | bytes 3145736 | tf_op jit(solution)/shard_map/ppermute | solution.py:295
  135.6 37.2 %collective-permute-start = (bf16[1024,256]{1,0:T(8,128)(2,1)S(1)}, bf16[1024,256]{1,0:T(8,128)(2,1)S(1)}, u32[]{:S(2)}, u32[]{:S(2)}) collective-permute-start(bf16[1024,256]{1,0:T(8,128)(2,1)S(1)} %copy-done.24), channel_id=1, source_target_pairs={{8,0},{16,8},{24,16},{0,24},{9,1},{17,9},{25,17},{1,25},{10,2},{18... | collective-permute-start | bytes 1572872 | tf_op jit(solution)/shard_map/ppermute | solution.py:295
  139.2 33.7 %collective-permute-start.5 = (bf16[1024,256]{1,0:T(8,128)(2,1)S(1)}, bf16[1024,256]{1,0:T(8,128)(2,1)}, u32[]{:S(2)}, u32[]{:S(2)}) collective-permute-start(bf16[1024,256]{1,0:T(8,128)(2,1)S(1)} %copy-done.25), channel_id=1, source_target_pairs={{16,0},{24,8},{0,16},{8,24},{17,1},{25,9},{1,17},{9,25},{18,2},{26... | collective-permute-start | bytes 1572872 | tf_op jit(solution)/shard_map/ppermute | solution.py:295
  139.2 36.3 %collective-permute-start.4 = (bf16[1024,256]{1,0:T(8,128)(2,1)S(1)}, bf16[1024,256]{1,0:T(8,128)(2,1)}, u32[]{:S(2)}, u32[]{:S(2)}) collective-permute-start(bf16[1024,256]{1,0:T(8,128)(2,1)S(1)} %copy-done.24), channel_id=1, source_target_pairs={{16,0},{24,8},{0,16},{8,24},{17,1},{25,9},{1,17},{9,25},{18,2},{26... | collective-permute-start | bytes 1572872 | tf_op jit(solution)/shard_map/ppermute | solution.py:295
  142.2 33.4 %collective-permute-start.10 = (bf16[1024,256]{1,0:T(8,128)(2,1)S(1)}, bf16[1024,256]{1,0:T(8,128)(2,1)S(1)}, u32[]{:S(2)}, u32[]{:S(2)}) collective-permute-start(bf16[1024,256]{1,0:T(8,128)(2,1)S(1)} %collective-permute-done.9.refs_9_), channel_id=1, source_target_pairs={{1,0},{2,1},{3,2},{0,3},{5,4},{6,5},{7,6},{4,7},{9,8},{10,9},{11,1... | collective-permute-start | bytes 1572872 | tf_op jit(solution)/shard_map/ppermute | solution.py:295
  175.5 22.4 %collective-permute-start.3 = (bf16[1024,256]{1,0:T(8,128)(2,1)S(1)}, bf16[1024,256]{1,0:T(8,128)(2,1)}, u32[]{:S(2)}, u32[]{:S(2)}) collective-permute-start(bf16[1024,256]{1,0:T(8,128)(2,1)S(1)} %collective-permute-done.refs_0_), channel_id=1, source_target_pairs={{3,0},{0,1},{1,2},{2,3},{7,4},{4,5},{5,6},{6,7},{11,8},{8,9},{9,10... | collective-permute-start | bytes 1572872 | tf_op jit(solution)/shard_map/ppermute | solution.py:295
  176.3 21.6 %collective-permute-start.6 = (bf16[1024,256]{1,0:T(8,128)(2,1)}, bf16[1024,256]{1,0:T(8,128)(2,1)}, u32[]{:S(2)}, u32[]{:S(2)}) collective-permute-start(bf16[1024,256]{1,0:T(8,128)(2,1)} %collective-permute-done.5.refs_5_), channel_id=1, source_target_pairs={{1,0},{2,1},{3,2},{0,3},{5,4},{6,5},{7,6},{4,7},{9,8},{10,9},{11,1... | collective-permute-start | bytes 1572872 | tf_op jit(solution)/shard_map/ppermute | solution.py:295
  179.0 30.2 %collective-permute-start.7 = (bf16[1024,256]{1,0:T(8,128)(2,1)}, bf16[1024,256]{1,0:T(8,128)(2,1)}, u32[]{:S(2)}, u32[]{:S(2)}) collective-permute-start(bf16[1024,256]{1,0:T(8,128)(2,1)} %collective-permute-done.4.refs_4_), channel_id=1, source_target_pairs={{3,0},{0,1},{1,2},{2,3},{7,4},{4,5},{5,6},{6,7},{11,8},{8,9},{9,10... | collective-permute-start | bytes 1572872 | tf_op jit(solution)/shard_map/ppermute | solution.py:295
  181.9 54.4 %all-to-all-start.2 = ((bf16[8,256,256]{2,1,0:T(8,128)(2,1)}), bf16[8,256,256]{2,1,0:T(8,128)(2,1)S(1)}, u32[]{:S(2)}, u32[]{:S(2)}) async-start(bf16[8,256,256]{2,1,0:T(8,128)(2,1)} %add_convert_fusion), calls=%async_computation.2 | async-start | bytes 2097152 | tf_op jit(solution)/shard_map/all_to_all | solution.py:349
  236.3 35.7 %all-to-all-start.1 = ((bf16[8,256,256]{2,1,0:T(8,128)(2,1)}), bf16[8,256,256]{2,1,0:T(8,128)(2,1)S(1)}, u32[]{:S(2)}, u32[]{:S(2)}) async-start(bf16[8,256,256]{2,1,0:T(8,128)(2,1)} %add_convert_fusion.1), calls=%async_computation.1 | async-start | bytes 2097152 | tf_op jit(solution)/shard_map/all_to_all | solution.py:349
  327.3 29.7 %all-to-all-start.3 = ((bf16[4,1024,256]{2,1,0:T(8,128)(2,1)}), bf16[4,1024,256]{2,1,0:T(8,128)(2,1)S(1)}, u32[]{:S(2)}, u32[]{:S(2)}) async-start(bf16[4,1024,256]{2,1,0:T(8,128)(2,1)} %broadcast_in_dim.64), calls=%async_computation.3 | async-start | bytes 4194304 | tf_op jit(solution)/shard_map/all_to_all | solution.py:259
  (32 other events, 198.5 us)

commit v2 on v0

v2 whole, which is shorter than its diff:
```python
import functools
import math

import jax
import jax.numpy as jnp
from jax import lax
from jax.experimental import pallas as pl
from jax.experimental.pallas import tpu as pltpu
from jax.sharding import Mesh
from jax.sharding import PartitionSpec as P

Z, X, C, Y = "dev_0", "dev_1", "dev_2", "rep"
DEV = (Z, X, C)
DEV_REP = (Z, X, C, Y)
AXES = {"z": Z, "x": X, "c": C, "y": Y}
MIB = 1024 * 1024

restart = 0.1
strength = 0.5
BF = jnp.bfloat16
F32 = jnp.float32
VMEM = pltpu.VMEM
SMEM = pltpu.SMEM


def vspec():
    return pl.BlockSpec(memory_space=VMEM)


def sspec():
    return pl.BlockSpec(memory_space=SMEM)


def aspec():
    return pl.BlockSpec(memory_space=pl.ANY)


def cost(flops, nbytes):
    return pl.CostEstimate(flops=int(flops), bytes_accessed=int(nbytes), transcendentals=0)


def pack_kernel(inv_ref, cnt_ref, tiles_ref, extra_ref, out_ref, sem):
    groups = out_ref.shape[0]
    for g in range(groups):
        for d in range(4):
            t = inv_ref[g * 4 + d]
            pltpu.make_async_copy(
                tiles_ref.at[t], out_ref.at[g, pl.ds(0, 128), pl.ds(d * 128, 128)], sem.at[g]
            ).start()
    lane = lax.broadcasted_iota(jnp.int32, (128, 128), 1)

    def one(g, carry):
        for d in range(4):
            pltpu.make_async_copy(
                tiles_ref.at[0], out_ref.at[g, pl.ds(0, 128), pl.ds(d * 128, 128)], sem.at[g]
            ).wait()
        for d in range(4):
            here = (pl.ds(0, 128), pl.ds(d * 128, 128))
            tile = out_ref[g, here[0], here[1]].astype(F32)
            tile = jnp.where(lane < cnt_ref[g * 4 + d], tile, 0.0)
            out_ref[g, here[0], here[1]] = tile.astype(BF)
        out_ref[g, 128:144, :] = extra_ref[g]
        return carry

    lax.fori_loop(0, groups, one, 0)


def packed_tiles(inv, cnt, tiles, extra):
    return pl.pallas_call(
        pack_kernel,
        out_shape=jax.ShapeDtypeStruct((16, 144, 512), BF),
        in_specs=[sspec(), sspec(), aspec(), vspec()],
        out_specs=vspec(),
        scratch_shapes=[pltpu.SemaphoreType.DMA((16,))],
        compiler_params=pltpu.CompilerParams(vmem_limit_bytes=16 * MIB),
        cost_estimate=cost(3e9, 5e6),
    )(inv, cnt, tiles, extra)


def rem(a, n):
    return lax.rem(a + n, n)


def step_kernel(
    idx_ref, pack_ref, hist_a_ref, hist_b_ref, tiles_ref, cols_ref, from_ref, prev_ref, zero_ref,
    weight_two_ref, weight_three_ref, grad_ref,
    three_ref, fresh_ref, term_ref,
    far, own_a, own_b, table, got, rows, vin, idx_in, idx, tiles, home, same, other, partner, sums,
    arrived_a, arrived_b, second, low, share, share_z, share_xc, share_y, whole, far_send, far_recv, y_send, y_recv, idx_send, idx_recv, v_send, v_recv,
    pair_send, pair_recv, sum_send, sum_recv, new_send, new_recv, local_sem,
    gz_send, gz_recv, gxc_send, gxc_recv, gy_send, gy_recv, hxc_send, hxc_recv, hz_send, hz_recv,
):
    z, x, core, turn = (lax.axis_index(a) for a in (Z, X, C, Y))
    hist = (hist_a_ref, hist_b_ref)
    own = (own_a, own_b)
    arrived = (arrived_a, arrived_b)

    def remote(src, dst, send, recv, **to):
        return pltpu.make_async_remote_copy(
            src_ref=src, dst_ref=dst, send_sem=send, recv_sem=recv,
            device_id={AXES[a]: v for a, v in to.items()},
            device_id_type=pl.DeviceIdType.MESH,
        )

    barrier = pltpu.get_barrier_semaphore()

    def greet(**to):
        pl.semaphore_signal(
            barrier, inc=1, device_id={AXES[a]: v for a, v in to.items()},
            device_id_type=pl.DeviceIdType.MESH,
        )

    for by in (1, 2, 3):
        greet(x=rem(x + by, 4))
        greet(x=rem(x + by, 4), c=1 - core)
        greet(y=rem(turn + by, 4))

    def greet_zc(o, carry):
        greet(z=rem(z + o // 2, 8), c=rem(core + o % 2, 2))
        return carry

    lax.fori_loop(1, 16, greet_zc, 0)

    local_copies = [
        pltpu.make_async_copy(hist[0], own_a, local_sem.at[0]),
        pltpu.make_async_copy(hist[1], own_b, local_sem.at[1]),
        pltpu.make_async_copy(tiles_ref.at[:, pl.ds(0, 4)], tiles, local_sem.at[2]),
        pltpu.make_async_copy(idx_ref.at[2 * z + core], idx_in.at[2 * z + core], local_sem.at[3]),
        pltpu.make_async_copy(pack_ref.at[2 * z + core], vin.at[2 * z + core], local_sem.at[4]),
    ]
    for copy in local_copies:
        copy.start()

    def quarter(l, q):
        return hist[l].at[pl.ds(rem(turn + q, 4) * 8, 8)]

    down, up = rem(x + 3, 4), rem(x + 1, 4)

    def along_x(l, n):
        d, q, src, to = (
            (0, 0, None, down), (0, 1, None, down), (2, 1, None, up), (2, 0, None, up),
            (1, 0, far.at[l, 0, 0], down), (1, 1, far.at[l, 2, 1], up),
        )[n]
        src = quarter(l, q) if src is None else src
        return remote(src, far.at[l, d, q], far_send.at[l, n], far_recv.at[l, d, q], x=to)

    def along_y(l, d, q):
        to, at = (rem(turn + 1, 4), 3) if q == 0 else (rem(turn + 3, 4), 2)
        return remote(
            far.at[l, d, q], far.at[l, d, at], y_send.at[l, d, q], y_recv.at[l, d, q], y=to
        )

    def x_here(l, d, q):
        remote(
            far.at[l, d, q], far.at[l, d, q], far_send.at[l, 0], far_recv.at[l, d, q], x=down
        ).wait_recv()

    def y_here(l, d):
        for q in range(2):
            along_y(l, d, q).wait_recv()

    def send_index(o):
        to_z, to_c = rem(z + o // 2, 8), rem(core + o % 2, 2)
        return remote(
            idx_ref.at[2 * to_z + to_c], idx_in.at[2 * z + core],
            idx_send.at[o], idx_recv.at[o], z=to_z, c=to_c,
        )

    def send_pack(o):
        to_z, to_c = rem(z + o // 2, 8), rem(core + o % 2, 2)
        return remote(
            pack_ref.at[2 * to_z + to_c], vin.at[2 * z + core],
            v_send.at[o], v_recv.at[o], z=to_z, c=to_c,
        )

    def each(first, last, act):
        def body(o, carry):
            act(o)
            return carry

        lax.fori_loop(first, last, body, 0)

    pl.semaphore_wait(barrier, 24)
    for n in (0, 2, 1, 3):
        along_x(0, n).start()
    each(1, 16, lambda o: send_index(o).start())
    each(1, 16, lambda o: send_pack(o).start())

    def gather(l, d):
        def widen(s, carry):
            r = pl.multiple_of(s * 128, 128)
            if d == 0:
                block = own[l][rem(s + 8 * turn, 32)]
            else:
                block = far[l, d - 1, s // 8, lax.rem(s, 8)]
            block = block.astype(F32)
            table[pl.ds(2 * r, 128, stride=2), :] = block[:, :128]
            table[pl.ds(2 * r + 1, 128, stride=2), :] = block[:, 128:]
            return carry

        lax.fori_loop(0, 32, widen, 0)

        def worker(g):
            for j in range(128):
                got[pl.ds(2 * j, 2), :] = table[pl.ds(2 * idx[g, d, j], 2), :]
            left, right = got[pl.ds(0, 128, stride=2), :], got[pl.ds(1, 128, stride=2), :]
            both = jnp.concatenate([left, right], axis=1).astype(BF)
            rows[l, g, pl.ds(d * 128, 128), :] = both

        each(0, 16, worker)

    def product(l, n, which):
        g = rem(z + n + 1, 8) * 2 + which
        packed = vin[g, 0:128, :]
        flag = vin[g, 128:129, :]
        both = jnp.concatenate([packed * flag, packed * (1 - flag)], axis=0)
        return jnp.dot(both, rows[l, g], preferred_element_type=F32)

    def to_partner(l, h):
        part = pl.ds(4 * h, 4)
        return remote(
            other.at[l, part], partner.at[l, part], pair_send.at[l, h], pair_recv.at[l, h],
            c=1 - core,
        )

    def send_sum(l, n):
        return remote(
            sums.at[l, pl.ds(2 * n, 2)], arrived[l].at[pl.ds(2 * n, 2)], sum_send.at[l, n], sum_recv.at[l, n],
            z=rem(z + n + 1, 8),
        )

    def plane_sums(l):
        for h in range(2):
            def for_partner(n):
                other[l, n] = product(l, n, 1 - core).astype(BF)

            each(4 * h, 4 * h + 4, for_partner)
            if h:
                to_partner(l, 0).start()

        def for_me(n):
            same[n] = product(l, n, core)

        each(0, 4, for_me)
        to_partner(l, 1).start()
        each(4, 8, for_me)

        def add(n):
            both = (same[n] + partner[l, n].astype(F32)).astype(BF)
            sums[l, pl.ds(2 * n, 2)] = both.reshape(2, 128, 256)

        to_partner(l, 0).wait_recv()
        add(0)

        def add_and_send(n):
            add(n)
            send_sum(l, n - 1).start()

        each(1, 4, add_and_send)
        to_partner(l, 1).wait_recv()
        each(4, 8, add_and_send)

    def at_home(l):
        def block_sum(i):
            total = None
            for t in range(l, 4):
                b = cols_ref[i, t]
                block = own[l][b] if t else prev_ref[b]
                part = jnp.dot(tiles[i, t], block, preferred_element_type=F32)
                total = part if total is None else total + part
            home[l, i] = total

        each(0, 8, block_sum)

    def finish(l, i):
        mine = pl.ds(pl.multiple_of(i * 128, 128), 128)
        total = home[l, i] + arrived[l][from_ref[i, 0]].astype(F32)
        total += arrived[l][from_ref[i, 1]].astype(F32)
        mixed = (1.0 - restart) * total + restart * zero_ref[mine, :].astype(F32)
        factor = math.log(strength / (l + 2) + 1.0)
        rounded = mixed.astype(BF)
        weight = (weight_two_ref, weight_three_ref)[l][...]
        out = jnp.dot(rounded, weight, preferred_element_type=F32)
        out = jnp.maximum((1.0 - factor) * mixed + factor * out, 0.0).astype(BF)
        return mine, rounded, out

    def relay(l):
        x_here(l, 0, 0)
        along_x(l, 4).start()
        along_y(l, 0, 0).start()
        x_here(l, 2, 1)
        along_x(l, 5).start()
        along_y(l, 2, 1).start()

    def second_pair(l):
        x_here(l, 2, 0)
        along_y(l, 2, 0).start()
        x_here(l, 0, 1)
        along_y(l, 0, 1).start()

    def third_pair(l):
        for q in range(2):
            x_here(l, 1, q)
            along_y(l, 1, q).start()

    def arrived_here(l):
        each(0, 7, lambda n: send_sum(l, n).wait_recv())

    for copy in local_copies:
        copy.wait()
    each(1, 16, lambda o: send_index(o).wait_recv())
    to_smem = pltpu.make_async_copy(idx_in, idx, local_sem.at[5])
    to_smem.start()
    to_smem.wait()
    gather(0, 0)
    relay(0)
    for n in (0, 2, 1, 3):
        along_x(1, n).start()
    at_home(0)
    second_pair(0)
    gather(1, 0)
    third_pair(0)
    y_here(0, 0)
    gather(0, 1)
    y_here(0, 2)
    gather(0, 3)
    relay(1)
    y_here(0, 1)
    gather(0, 2)
    each(1, 16, lambda o: send_pack(o).wait_recv())
    plane_sums(0)
    second_pair(1)
    at_home(1)
    third_pair(1)
    y_here(1, 0)
    gather(1, 1)
    y_here(1, 2)
    gather(1, 3)
    arrived_a[14:16] = sums[0, 14:16]
    arrived_here(0)

    def layer_two(i):
        second[i] = finish(0, i)[2]

    each(0, 8, layer_two)
    y_here(1, 1)
    gather(1, 2)
    plane = fresh_ref.at[pl.ds(turn * 8, 8)]
    new_copies = [
        remote(second, plane, new_send.at[s - 1], new_recv.at[s - 1], y=rem(turn + s, 4))
        for s in (1, 2, 3)
    ]
    plane_sums(1)
    for copy in new_copies:
        copy.start()
    keep = pltpu.make_async_copy(second, plane, local_sem.at[6])
    keep.start()

    def add_current(i):
        block = second[cols_ref[i, 0]]
        home[1, i] += jnp.dot(tiles[i, 0], block, preferred_element_type=F32)

    each(0, 8, add_current)
    arrived_b[14:16] = sums[1, 14:16]
    arrived_here(1)

    def layer_three(i):
        mine, rounded, out = finish(1, i)
        three_ref[mine, :] = out
        low[mine, :] = rounded

    each(0, 8, layer_three)
    term = math.log(strength / 3 + 1.0) * lax.dot_general(
        low[...], grad_ref[...], (((0,), (0,)), ((), ())), preferred_element_type=F32
    )
    share[0:32] = term[:, :128].reshape(32, 8, 128)
    share[32:64] = term[:, 128:].reshape(32, 8, 128)
    for copy in new_copies:
        copy.wait_recv()
    keep.wait()

    def xc(o):
        return rem(x + o // 2, 4), rem(core + o % 2, 2)

    def term_z(dz):
        to = rem(z + dz, 8)
        return remote(
            share.at[pl.ds(8 * to, 8)], share_z.at[dz], gz_send.at[dz], gz_recv.at[dz], z=to
        )

    def term_xc(o):
        to_x, to_c = xc(o)
        return remote(
            share_z.at[0, 2 * to_x + to_c], share_xc.at[o], gxc_send.at[o], gxc_recv.at[o],
            x=to_x, c=to_c,
        )

    def term_y(dy):
        return remote(
            share_xc.at[0], share_y.at[turn], gy_send.at[dy], gy_recv.at[dy],
            y=rem(turn + dy, 4),
        )

    mine = 8 * z + 2 * x + core

    def back_xc(o):
        to_x, to_c = xc(o)
        return remote(
            whole.at[mine], whole.at[mine], hxc_send.at[o], hxc_recv.at[o], x=to_x, c=to_c
        )

    def back_z(dz):
        plane = whole.at[pl.ds(8 * z, 8)]
        return remote(plane, plane, hz_send.at[dz], hz_recv.at[dz], z=rem(z + dz, 8))

    each(1, 8, lambda o: term_z(o).start())
    each(1, 8, lambda o: term_z(o).wait_recv())
    total = share[pl.ds(8 * z, 8)]
    for o in range(1, 8):
        total += share_z[o]
    share_z[0] = total
    each(1, 8, lambda o: term_xc(o).start())
    each(1, 8, lambda o: term_xc(o).wait_recv())
    total = share_z[0, 2 * x + core]
    for o in range(1, 8):
        total += share_xc[o]
    share_xc[0] = total
    share_y[turn] = total
    each(1, 4, lambda o: term_y(o).start())
    each(1, 4, lambda o: term_y(o).wait_recv())
    whole[mine] = share_y[0] + share_y[1] + share_y[2] + share_y[3]
    each(1, 8, lambda o: back_xc(o).start())
    each(1, 8, lambda o: back_xc(o).wait_recv())
    each(1, 8, lambda o: back_z(o).start())
    each(1, 8, lambda o: back_z(o).wait_recv())
    term_ref[:, :128] = whole[0:32].reshape(256, 128)
    term_ref[:, 128:] = whole[32:64].reshape(256, 128)
    for copy in (term_z, term_xc, back_xc, back_z):
        each(1, 8, lambda o: copy(o).wait_send())
    each(1, 4, lambda o: term_y(o).wait_send())
    for l in range(2):
        for n in range(6):
            along_x(l, n).wait_send()
        for d in range(3):
            for q in range(2):
                along_y(l, d, q).wait_send()
        for h in range(2):
            to_partner(l, h).wait_send()
        each(0, 7, lambda n: send_sum(l, n).wait_send())
    each(1, 16, lambda o: send_index(o).wait_send())
    each(1, 16, lambda o: send_pack(o).wait_send())
    for copy in new_copies:
        copy.wait_send()


def whole_step(*args):
    dma = pltpu.SemaphoreType.DMA
    return pl.pallas_call(
        step_kernel,
        out_shape=(
            jax.ShapeDtypeStruct((1024, 256), BF),
            jax.ShapeDtypeStruct((32, 128, 256), BF),
            jax.ShapeDtypeStruct((256, 256), F32),
        ),
        in_specs=[aspec(), aspec(), aspec(), aspec(), aspec(), sspec(), sspec()] + [vspec()] * 5,
        out_specs=(vspec(), aspec(), vspec()),
        scratch_shapes=[
            VMEM((2, 3, 4, 8, 128, 256), BF),
            VMEM((32, 128, 256), BF),
            VMEM((32, 128, 256), BF),
            VMEM((8192, 128), F32),
            VMEM((256, 128), F32),
            VMEM((2, 16, 512, 256), BF),
            VMEM((16, 144, 512), BF),
            VMEM((16, 4, 128), jnp.int32),
            SMEM((16, 4, 128), jnp.int32),
            VMEM((8, 4, 128, 128), BF),
            VMEM((2, 8, 128, 256), F32),
            VMEM((8, 256, 256), F32),
            VMEM((2, 8, 256, 256), BF),
            VMEM((2, 8, 256, 256), BF),
            VMEM((2, 16, 128, 256), BF),
            VMEM((16, 128, 256), BF),
            VMEM((16, 128, 256), BF),
            VMEM((8, 128, 256), BF),
            VMEM((1024, 256), BF),
            VMEM((64, 8, 128), F32),
            VMEM((8, 8, 8, 128), F32),
            VMEM((8, 8, 128), F32),
            VMEM((4, 8, 128), F32),
            VMEM((64, 8, 128), F32),
            dma((2, 6)), dma((2, 3, 2)), dma((2, 3, 2)), dma((2, 3, 2)),
            dma((16,)), dma((16,)), dma((16,)), dma((16,)),
            dma((2, 2)), dma((2, 2)), dma((2, 7)), dma((2, 7)), dma((3,)), dma((3,)), dma((7,)),
            dma((8,)), dma((8,)), dma((8,)), dma((8,)), dma((4,)), dma((4,)),
            dma((8,)), dma((8,)), dma((8,)), dma((8,)),
        ],
        compiler_params=pltpu.CompilerParams(
            vmem_limit_bytes=60 * MIB, collective_id=1, has_side_effects=True
        ),
        cost_estimate=cost(60e9, 40e6),
    )(*args)


def local(
    h_zero, h_prev, hist_a, hist_b, tile_vals, tile_cols, pull_rows, pull_counts,
    weight_two, weight_three, grad_out,
):
    x, turn = lax.axis_index(X), lax.axis_index(Y)

    k = lax.broadcasted_iota(jnp.int32, (8, 2, 4), 0)
    c = lax.broadcasted_iota(jnp.int32, (8, 2, 4), 1)
    d = lax.broadcasted_iota(jnp.int32, (8, 2, 4), 2)
    owner = (8 * k + 2 * lax.rem(x + d, 4) + c).reshape(64)
    named = tile_cols[:, 4:].reshape(64) - 40
    block = lax.broadcasted_iota(jnp.int32, (8, 8), 0).reshape(64)
    place = (lax.broadcasted_iota(jnp.int32, (8, 8), 1) + 12 * block.reshape(8, 8) + 4).reshape(64)
    is_it = named[None, :] == jnp.arange(64, dtype=jnp.int32)[:, None]
    tile_of = jnp.sum(jnp.where(is_it, place[None, :], 0), axis=1)
    block_of = jnp.sum(jnp.where(is_it, block[None, :], 0), axis=1).reshape(8, 8)
    ends = jnp.stack([block_of[:, 0], block_of[:, 7]], axis=1)
    first = (block_of == ends[:, :1]).reshape(64)
    inv = jnp.take(tile_of, owner)
    cnt = jnp.take(pull_counts[0], owner)
    rows = lax.rem(jnp.take(pull_rows[0], owner, axis=0) + (4096 - 1024 * turn), 4096)
    flag = jnp.broadcast_to(jnp.take(first, owner)[:, None], (64, 128)).reshape(16, 1, 512)
    extra = jnp.pad(flag.astype(BF), ((0, 0), (0, 15), (0, 0)))
    tiles = packed_tiles(inv, cnt, tile_vals.reshape(96, 128, 128), extra)
    blocks = jnp.arange(8, dtype=jnp.int32)
    plane = jnp.sum(
        jnp.where(ends[:, :, None] == blocks[None, None, :], blocks[:, None, None], 0), axis=0
    ).T
    slots = 2 * lax.rem(lax.axis_index(Z) - plane - 1 + 16, 8) + jnp.arange(2, dtype=jnp.int32)
    near = tile_cols[:, :4] - jnp.array([0, 8, 8, 8], dtype=jnp.int32)
    layer_three, fresh_rows, grad_total = whole_step(
        rows.reshape(16, 4, 128), tiles, hist_a.reshape(32, 128, 256),
        hist_b.reshape(32, 128, 256), tile_vals, near, slots,
        h_prev.reshape(8, 128, 256), h_zero, weight_two, weight_three, grad_out,
    )
    return (layer_three, fresh_rows.reshape(4096, 256), grad_total)


def solution(mesh):
    finer = Mesh(mesh.devices.reshape(8, 4, 2, mesh.shape["rep"]), (Z, X, C, Y))
    return jax.shard_map(
        local,
        mesh=finer,
        in_specs=(
            P(DEV_REP, None),
            P(DEV_REP, None),
            P(DEV, None),
            P(DEV, None),
            P(DEV_REP, None, None, None),
            P(DEV_REP, None),
            P(DEV_REP, None, None),
            P(DEV_REP, None),
            P(),
            P(),
            P(DEV_REP, None),
        ),
        out_specs=(P(DEV_REP, None), P(DEV, None), P()),
        check_vma=False,
    )
```

time: 471 us -> 191 us (0.41)
  waiting for transfers between devices: 206 us -> 0 us
  Pallas kernels: 0 us -> 171 us
  local copies, waits for them, and re-layouts: 92.9 us -> 15.1 us
  other arithmetic: 80.1 us -> 3.88 us
  blocking collectives: 74.9 us -> 0 us
  starting transfers between devices: 10.4 us -> 0 us
  matrix products: 5.81 us -> 0 us
    all_to_all x2 -> x0, waiting for transfers between devices: 206 us -> none  [the longest x1 183 us: in_one_piece(): lax.all_to_all(both, axis, split_axis=split_dim, concat_axis=concat_dim,...]
    pallas_call x0 -> x2, Pallas kernels: none -> 171 us  [the longest x1 169 us: whole_step(): pl.pallas_call(step_kernel, out_shape=(jax.ShapeDtypeStruct((1024, 256),...]
    gather x4 -> x5, local copies, waits for them, and re-layouts: 83.8 us -> 3.68 us  [the longest x1 1.43 us: local(): cnt = jnp.take(pull_counts[0], owner)]
    all_to_all x5 -> x0, blocking collectives: 74.9 us -> none  [the longest x2 23.9 us: sent_to_all(): return lax.all_to_all(copies, axis, split_axis=0, concat_axis=0, tiled=True)]
    concatenate x3 -> x0, other arithmetic: 55.6 us -> none  [the longest x2 47.9 us: propagate(): jnp.concatenate([current, history, pulled.reshape(-1, feature_width)], ax...]
    select_n x5 -> x3, other arithmetic: 24.1 us -> 0.03 us  [the longest x1 0.01 us: local(): inv = jnp.take(tile_of, owner)]
    all_to_all x2 -> x0, starting transfers between devices: 10.4 us -> none  [the longest x1 5.94 us: in_one_piece(): lax.all_to_all(both, axis, split_axis=split_dim, concat_axis=concat_dim,...]
    dot_general x5 -> x0, matrix products: 5.81 us -> none  [the longest x2 3.02 us: propagate(): product = jnp.dot(mixed_low, weight, preferred_element_type=jnp.float32)]
  transfers between devices with their start and end apart: 2 -> 0, of which waited for: 2 -> 0; matrix products, arithmetic and copies ran while one was open for 1% -> 0% of each run, Pallas kernels for 0% -> 0%
where the time goes in v2:
time: 191 us
  Pallas kernels  171 us (90%)
  local copies, waits for them, and re-layouts  15.1 us (8%)
  other arithmetic  3.88 us (2%)
    pallas_call x1, Pallas kernels, whole_step(): pl.pallas_call(step_kernel, out_shape=(jax.ShapeDtypeStruct((1024, 256),...  169 us
    unnamed x11, local copies, waits for them, and re-layouts  9.7 us

profile of v2, /device:TPU:1, one launch (start us, length us, event | category | flops | bytes accessed | tf_op | source)
XLA Modules:
  0.0 191.0 jit_solution(5917983085229328764)
XLA Ops:
  0.7 0.7 copy-done
  1.7 1.3 slice_add_fusion.cols_ref
  3.0 0.8 slice_add_fusion.1
  3.9 0.1 select_reduce_fusion
  4.1 0.1 fusion.17
  4.6 0.6 fusion.6.from_ref
  5.5 0.1 iota.105
  5.6 0.1 iota.97
  5.7 0.1 iota.106
  5.8 0.1 iota.99
  6.0 0.8 gather_fusion.2
  6.8 1.4 gather_fusion.3
  8.2 0.1 iota.101
  8.3 0.8 gather_fusion.1
  9.1 0.1 gather.18
  9.4 0.6 gather_fusion
  10.0 0.7 negate_select_fusion.idx_ref
  10.8 1.9 copy-done.1
  12.7 1.9 shard_map.139.pack_ref
  14.5 1.4 copy-done.2
  15.9 169.4 %shard_map.140 = (bf16[1024,256]{1,0:T(8,128)(2,1)}, bf16[32,128,256]{2,1,0:T(8,128)(2,1)}, f32[256,256]{1,0:T(8,128)}) custom-call(s32[16,4,128]{2,1,0:T(4,128)} %negate_select_fusion.idx_ref, bf16[16,144,512]{2,1,0:T(8,128)(2,1)} %copy-done.2, bf16[32,128,256]{2,1,0:T(8,128)(2,1)} %bitcast.19, bf16[32,128,256]{2,1,0:T(8,128)(2,1)} %bitcast.20, ...), custom_call_target="tpu_custom_call" | custom-call | flops 60000002048 | bytes 40000000 | tf_op jit(solution)/shard_map/pallas_call | solution.py:458
  185.4 1.9 copy.26
  187.2 3.1 %copy.27 = bf16[4096,256]{1,0:T(8,128)(2,1)} copy(bf16[4096,256]{1,0:T(8,128)(2,1)} %bitcast.16) | data formatting | bytes 4194304
  190.3 0.7 copy.28
  (39 shorter events, 1.5 us)
Async XLA Ops:
  0.6 0.8 copy-start
  10.8 1.9 copy-start.1
  14.5 1.4 copy-start.2
  187.2 3.1 %copy-start.3 = (f32[256,256]{1,0:T(8,128)S(1)}, f32[256,256]{1,0:T(8,128)}, u32[]{:S(2)}) copy-start(f32[256,256]{1,0:T(8,128)} %get-tuple-element.26) | copy-start | bytes 786436

commit v3 on v2

v3 whole, which is shorter than its diff:
```python
import functools
import math

import jax
import jax.numpy as jnp
from jax import lax
from jax.experimental import pallas as pl
from jax.experimental.pallas import tpu as pltpu
from jax.sharding import Mesh
from jax.sharding import PartitionSpec as P

Z, X, C, Y = "dev_0", "dev_1", "dev_2", "rep"
DEV = (Z, X, C)
DEV_REP = (Z, X, C, Y)
AXES = {"z": Z, "x": X, "c": C, "y": Y}
MIB = 1024 * 1024
PIECES = 4

restart = 0.1
strength = 0.5
BF = jnp.bfloat16
F32 = jnp.float32
VMEM = pltpu.VMEM
SMEM = pltpu.SMEM


def vspec():
    return pl.BlockSpec(memory_space=VMEM)


def sspec():
    return pl.BlockSpec(memory_space=SMEM)


def aspec():
    return pl.BlockSpec(memory_space=pl.ANY)


def cost(flops, nbytes):
    return pl.CostEstimate(flops=int(flops), bytes_accessed=int(nbytes), transcendentals=0)


def table_kernel(cols_ref, tile_ref, first_ref, near_ref, slots_ref, owner_block):
    z = lax.axis_index(Z)

    def name(i, carry):
        near_ref[i, 0] = cols_ref[i, 0]
        for t in range(1, 4):
            near_ref[i, t] = cols_ref[i, t] - 8
        for t in range(4, 12):
            p = cols_ref[i, t] - 40
            tile_ref[p] = 12 * i + t
            owner_block[p] = i
        return carry

    lax.fori_loop(0, 8, name, 0)

    def plane(k, carry):
        on = lax.rem(z - k + 8, 8)
        place = jnp.where(on == 0, 7, jnp.where(on == 4, 0, on - on // 5))
        i = owner_block[8 * k]
        slots_ref[i, 0] = 2 * place
        slots_ref[owner_block[8 * k + 7], 1] = 2 * place + 1
        for n in range(8):
            first_ref[8 * k + n] = jnp.where(owner_block[8 * k + n] == i, 1, 0)
        return carry

    lax.fori_loop(0, 8, plane, 0)


def tables(cols):
    return pl.pallas_call(
        table_kernel,
        out_shape=[
            jax.ShapeDtypeStruct(shape, jnp.int32) for shape in ((64,), (64,), (8, 4), (8, 2))
        ],
        in_specs=[sspec()],
        out_specs=[sspec()] * 4,
        scratch_shapes=[SMEM((64,), jnp.int32)],
    )(cols)


def publish_kernel(n, *refs):
    ins, outs, held, sems = refs[:n], refs[n : 2 * n], refs[2 * n : 3 * n], refs[3 * n]
    into = [pltpu.make_async_copy(i, h, sems.at[0, k]) for k, (i, h) in enumerate(zip(ins, held))]
    onto = [pltpu.make_async_copy(h, o, sems.at[1, k]) for k, (h, o) in enumerate(zip(held, outs))]
    for copy in into:
        copy.start()
    for first, then in zip(into, onto):
        first.wait()
        then.start()
    for copy in onto:
        copy.wait()


def published(*arrays):
    shapes = [jax.ShapeDtypeStruct(a.shape, a.dtype) for a in arrays]
    n = len(arrays)
    return pl.pallas_call(
        functools.partial(publish_kernel, n),
        out_shape=shapes,
        in_specs=[aspec()] * n,
        out_specs=[aspec()] * n,
        scratch_shapes=[VMEM(a.shape, a.dtype) for a in arrays] + [pltpu.SemaphoreType.DMA((2, n))],
        compiler_params=pltpu.CompilerParams(vmem_limit_bytes=63 * MIB),
        cost_estimate=cost(1e6, 6e6),
    )(*arrays)


def rem(a, n):
    return lax.rem(a + n, n)


def step_kernel(
    tile_ref, first_ref, cols_ref, from_ref, cnt_ref, pull_ref, weight_two_ref, weight_three_ref,
    hist_a_ref, hist_b_ref, tiles_hbm, prev_hbm, zero_hbm, grad_hbm,
    three_ref, fresh_ref, term_ref,
    far, own_a, own_b, prev_ref, zero_ref, grad_ref, table, got, rows, pack_ref, vin, idx_ref, idx_in,
    idx, tiles, home, same, other, partner, sums,
    arrived_a, arrived_b, second, low, three, share, share_c, share_xy, share_z, whole, v_mid, s_mid,
    far_send, far_recv, y_send, y_recv, idx_send, idx_recv, v_send, v_recv,
    pair_send, pair_recv, sum_send, sum_recv, new_send, new_recv, local_sem,
    far_z_send, far_z_recv, gc_sem, gxy_send, gxy_recv, gz_send, gz_recv, hxy_send, hxy_recv,
):
    z, x, core, turn = (lax.axis_index(a) for a in (Z, X, C, Y))
    hist = (hist_a_ref, hist_b_ref)
    own = (own_a, own_b)
    arrived = (arrived_a, arrived_b)

    def remote(src, dst, send, recv, **to):
        return pltpu.make_async_remote_copy(
            src_ref=src, dst_ref=dst, send_sem=send, recv_sem=recv,
            device_id={AXES[a]: v for a, v in to.items()},
            device_id_type=pl.DeviceIdType.MESH,
        )

    barrier = pltpu.get_barrier_semaphore()

    def greet(**to):
        pl.semaphore_signal(
            barrier, inc=1, device_id={AXES[a]: v for a, v in to.items()},
            device_id_type=pl.DeviceIdType.MESH,
        )

    def greet_zc(o, carry):
        greet(z=rem(z + o // 2, 8), c=rem(core + o % 2, 2))
        greet(x=rem(x + o // 4, 4), y=rem(turn + o % 4, 4))
        return carry

    lax.fori_loop(1, 16, greet_zc, 0)

    local_copies = [
        pltpu.make_async_copy(hist[0], own_a, local_sem.at[0]),
        pltpu.make_async_copy(hist[1], own_b, local_sem.at[1]),
        pltpu.make_async_copy(prev_hbm, prev_ref, local_sem.at[3]),
        pltpu.make_async_copy(zero_hbm, zero_ref, local_sem.at[4]),
        pltpu.make_async_copy(grad_hbm, grad_ref, local_sem.at[7]),
    ]
    tiles_copy = pltpu.make_async_copy(tiles_hbm, tiles, local_sem.at[2])
    tiles_copy.start()
    for copy in local_copies:
        copy.start()

    def owner(g, d):
        return 8 * (g // 2) + 2 * lax.rem(x + d, 4) + lax.rem(g, 2)

    def want(g, carry):
        for d in range(4):
            p = owner(g, d)
            row = pull_ref[pl.ds(p, 1), :] + (4096 - 1024 * turn)
            idx_ref[g, d : d + 1, :] = lax.rem(row, 4096)
            idx_ref[g, 4 + d : 5 + d, :] = jnp.full((1, 128), first_ref[p], jnp.int32)
        return carry

    lax.fori_loop(0, 16, want, 0)

    lane = lax.broadcasted_iota(jnp.int32, (128, 128), 1)

    def pack(g, carry):
        for d in range(4):
            p = owner(g, d)
            tile = tiles[tile_ref[p]].astype(F32)
            tile = jnp.where(lane < cnt_ref[0, p], tile, 0.0).astype(BF)
            pack_ref[g, :, d * 128 : (d + 1) * 128] = tile
        return carry

    size = 8 // PIECES
    down, up = rem(x + 3, 4), rem(x + 1, 4)

    def piece(l, d, q, h):
        return far.at[l, d, q, pl.ds(h * size, size)]

    def along_x(l, n, h):
        d, q, relayed, to = (
            (0, 0, None, down), (0, 1, None, down), (2, 1, None, up), (2, 0, None, up),
            (1, 0, (0, 0), down), (1, 1, (2, 1), up),
        )[n]
        if relayed is None:
            src = hist[l].at[pl.ds(rem(turn + q, 4) * 8 + h * size, size)]
        else:
            src = piece(l, *relayed, h)
        return remote(
            src, piece(l, d, q, h), far_send.at[l, n, h], far_recv.at[l, 2 * d + q, h], x=to
        )

    def along_y(l, d, q, h):
        to, at = (rem(turn + 1, 4), 3) if q == 0 else (rem(turn + 3, 4), 2)
        return remote(
            piece(l, d, q, h), piece(l, d, at, h),
            y_send.at[l, 2 * d + q, h], y_recv.at[l, 2 * d + q, h], y=to,
        )

    def x_here(l, d, q, h):
        remote(
            piece(l, d, q, h), piece(l, d, q, h),
            far_send.at[l, 0, h], far_recv.at[l, 2 * d + q, h], x=down,
        ).wait_recv()

    def y_here(l, d):
        for q in range(2):
            for h in range(PIECES):
                along_y(l, d, q, h).wait_recv()

    def own_rows(l):
        for n in (0, 2, 1, 3):
            for h in range(PIECES):
                along_x(l, n, h).start()

    def send_index(o):
        to_z, to_c = rem(z + o // 2, 8), rem(core + o % 2, 2)
        return remote(
            idx_ref.at[2 * to_z + to_c], idx_in.at[2 * z + core],
            idx_send.at[o], idx_recv.at[o], z=to_z, c=to_c,
        )

    def send_pack(o):
        to_z, to_c = rem(z + o // 2, 8), rem(core + o % 2, 2)
        return remote(
            pack_ref.at[2 * to_z + to_c], vin.at[2 * z + core],
            v_send.at[o], v_recv.at[o], z=to_z, c=to_c,
        )

    def pack_out(s):
        to_c = (core, 1 - core)[s]
        return remote(
            pack_ref.at[2 * rem(z + 4, 8) + to_c], v_mid.at[s],
            far_z_send.at[0, s], far_z_recv.at[0, s], z=rem(z + (1, 7)[s], 8),
        )

    def pack_on(s):
        source = rem(z + (7, 1)[s], 8)
        return remote(
            v_mid.at[s], vin.at[2 * source + core],
            v_send.at[8 + s], v_recv.at[8 + s], z=rem(source + 4, 8), c=(core, 1 - core)[s],
        )

    def sum_out(l, s):
        return remote(
            sums.at[l, s], s_mid.at[l, s],
            far_z_send.at[1 + l, s], far_z_recv.at[1 + l, s], z=rem(z + (1, 7)[s], 8),
        )

    def sum_on(l, s):
        return remote(
            s_mid.at[l, s], arrived[l].at[s],
            sum_send.at[l, 7 * s], sum_recv.at[l, 7 * s], z=rem(z + (3, 5)[s], 8),
        )

    def packs(act):
        each(2, 8, act)
        each(10, 16, act)
        act(1)

    def pass_packs():
        for s in range(2):
            pack_out(s).wait_recv()
            pack_on(s).start()

    def pass_sums(l):
        for s in range(2):
            sum_out(l, s).wait_recv()
            sum_on(l, s).start()

    def each(first, last, act):
        def body(o, carry):
            act(o)
            return carry

        lax.fori_loop(first, last, body, 0)

    pl.semaphore_wait(barrier, 30)
    own_rows(0)
    each(1, 16, lambda o: send_index(o).start())
    tiles_copy.wait()
    lax.fori_loop(0, 16, pack, 0)
    idx_in[2 * z + core] = idx_ref[2 * z + core]
    vin[2 * z + core] = pack_ref[2 * z + core]
    for s in range(2):
        pack_out(s).start()
    packs(lambda o: send_pack(o).start())

    def gather(l, d):
        def widen(s, carry):
            r = pl.multiple_of(s * 128, 128)
            if d == 0:
                block = own[l][rem(s + 8 * turn, 32)]
            else:
                block = far[l, d - 1, s // 8, lax.rem(s, 8)]
            block = block.astype(F32)
            table[pl.ds(2 * r, 128, stride=2), :] = block[:, :128]
            table[pl.ds(2 * r + 1, 128, stride=2), :] = block[:, 128:]
            return carry

        lax.fori_loop(0, 32, widen, 0)

        def worker(g):
            for j in range(128):
                got[pl.ds(2 * j, 2), :] = table[pl.ds(2 * idx[g, d, j], 2), :]
            left, right = got[pl.ds(0, 128, stride=2), :], got[pl.ds(1, 128, stride=2), :]
            both = jnp.concatenate([left, right], axis=1).astype(BF)
            rows[l, g, pl.ds(d * 128, 128), :] = both

        each(0, 16, worker)

    def away(n):
        return lax.rem(n + n // 4 + 4 * ((8 - n) // 8), 8)

    def product(l, n, which):
        g = rem(z + away(n), 8) * 2 + which
        packed = vin[g]
        flag = jnp.concatenate([idx_in[g, 4 + d : 5 + d, :] for d in range(4)], axis=1)
        flag = flag.astype(F32).astype(BF)
        both = jnp.concatenate([packed * flag, packed * (1 - flag)], axis=0)
        return jnp.dot(both, rows[l, g], preferred_element_type=F32)

    def to_partner(l, h):
        part = pl.ds(4 * h, 4)
        return remote(
            other.at[l, part], partner.at[l, part], pair_send.at[l, h], pair_recv.at[l, h],
            c=1 - core,
        )

    def send_sum(l, n):
        return remote(
            sums.at[l, pl.ds(2 * n, 2)], arrived[l].at[pl.ds(2 * n, 2)], sum_send.at[l, n], sum_recv.at[l, n],
            z=rem(z + away(n), 8),
        )

    def plane_sums(l):
        for h in range(2):
            def for_partner(n):
                other[l, n] = product(l, n, 1 - core).astype(BF)

            each(4 * h, 4 * h + 4, for_partner)
            if h:
                to_partner(l, 0).start()

        def for_me(n):
            same[n] = product(l, n, core)

        each(0, 4, for_me)
        to_partner(l, 1).start()
        each(4, 8, for_me)

        def add(n):
            both = (same[n] + partner[l, n].astype(F32)).astype(BF)
            sums[l, pl.ds(2 * n, 2)] = both.reshape(2, 128, 256)

        to_partner(l, 0).wait_recv()
        add(0)
        add(1)
        for s in range(2):
            sum_out(l, s).start()

        def add_and_send(n):
            add(n)
            send_sum(l, n - 1).start()

        each(2, 4, add_and_send)
        to_partner(l, 1).wait_recv()
        each(4, 8, add_and_send)

    def at_home(l):
        def block_sum(i):
            total = None
            for t in range(l, 4):
                b = cols_ref[i, t]
                block = own[l][b] if t else prev_ref[b]
                part = jnp.dot(tiles[12 * i + t], block, preferred_element_type=F32)
                total = part if total is None else total + part
            home[l, i] = total

        each(0, 8, block_sum)

    def finish(l, i):
        mine = pl.ds(pl.multiple_of(i * 128, 128), 128)
        total = home[l, i] + arrived[l][from_ref[i, 0]].astype(F32)
        total += arrived[l][from_ref[i, 1]].astype(F32)
        mixed = (1.0 - restart) * total + restart * zero_ref[mine, :].astype(F32)
        factor = math.log(strength / (l + 2) + 1.0)
        rounded = mixed.astype(BF)
        weight = (weight_two_ref, weight_three_ref)[l][...]
        out = jnp.dot(rounded, weight, preferred_element_type=F32)
        out = jnp.maximum((1.0 - factor) * mixed + factor * out, 0.0).astype(BF)
        return mine, rounded, out

    def relay(l):
        for h in range(PIECES):
            for n, d, q in ((4, 0, 0), (5, 2, 1)):
                x_here(l, d, q, h)
                along_x(l, n, h).start()
                along_y(l, d, q, h).start()

    def pass_on(l, *pairs):
        for h in range(PIECES):
            for d, q in pairs:
                x_here(l, d, q, h)
                along_y(l, d, q, h).start()

    def second_pair(l):
        pass_on(l, (2, 0), (0, 1))

    def third_pair(l):
        pass_on(l, (1, 0), (1, 1))

    def arrived_here(l):
        each(1, 7, lambda n: send_sum(l, n).wait_recv())
        for s in range(2):
            sum_on(l, s).wait_recv()

    for copy in local_copies:
        copy.wait()
    each(1, 16, lambda o: send_index(o).wait_recv())
    to_smem = pltpu.make_async_copy(idx_in, idx, local_sem.at[5])
    to_smem.start()
    to_smem.wait()
    relay(0)
    own_rows(1)
    gather(0, 0)
    at_home(0)
    pass_packs()
    second_pair(0)
    gather(1, 0)
    third_pair(0)
    y_here(0, 0)
    gather(0, 1)
    y_here(0, 2)
    gather(0, 3)
    relay(1)
    y_here(0, 1)
    gather(0, 2)
    packs(lambda o: send_pack(o).wait_recv())
    for s in range(2):
        pack_on(s).wait_recv()
    plane_sums(0)
    second_pair(1)
    at_home(1)
    pass_sums(0)
    third_pair(1)
    y_here(1, 0)
    gather(1, 1)
    y_here(1, 2)
    gather(1, 3)
    y_here(1, 1)
    gather(1, 2)
    plane_sums(1)
    arrived_a[14:16] = sums[0, 14:16]
    arrived_here(0)

    def layer_two(i):
        second[i] = finish(0, i)[2]

    each(0, 8, layer_two)
    pass_sums(1)
    plane = fresh_ref.at[pl.ds(turn * 8, 8)]
    new_copies = [
        remote(second, plane, new_send.at[s - 1], new_recv.at[s - 1], y=rem(turn + s, 4))
        for s in (1, 2, 3)
    ]
    for copy in new_copies:
        copy.start()
    keep = pltpu.make_async_copy(second, plane, local_sem.at[6])
    keep.start()

    def add_current(i):
        block = second[cols_ref[i, 0]]
        home[1, i] += jnp.dot(tiles[12 * i], block, preferred_element_type=F32)

    each(0, 8, add_current)
    arrived_b[14:16] = sums[1, 14:16]
    arrived_here(1)

    def layer_three(i):
        mine, rounded, out = finish(1, i)
        three[mine, :] = out
        low[mine, :] = rounded

    each(0, 8, layer_three)
    three_copy = pltpu.make_async_copy(three, three_ref, local_sem.at[1])
    term = math.log(strength / 3 + 1.0) * lax.dot_general(
        low[...], grad_ref[...], (((0,), (0,)), ((), ())), preferred_element_type=F32
    )
    share[0:32] = term[:, :128].reshape(32, 8, 128)
    share[32:64] = term[:, 128:].reshape(32, 8, 128)
    three_copy.start()
    for copy in new_copies:
        copy.wait_recv()
    keep.wait()

    half, theirs = pl.ds(32 * core, 32), pl.ds(32 * (1 - core), 32)
    place = 2 * (4 * x + turn)

    def xy(o):
        return rem(x + o // 4, 4), rem(turn + o % 4, 4)

    def term_c():
        return remote(share.at[theirs], share_c, gc_sem.at[0], gc_sem.at[1], c=1 - core)

    def term_xy(o):
        to_x, to_y = xy(o)
        return remote(
            share_c.at[pl.ds(2 * (4 * to_x + to_y), 2)], share_xy.at[o],
            gxy_send.at[o], gxy_recv.at[o], x=to_x, y=to_y,
        )

    def term_z(dz):
        return remote(
            share_xy.at[0], share_z.at[z], gz_send.at[dz], gz_recv.at[dz], z=rem(z + dz, 8)
        )

    def back_xy(o):
        to_x, to_y = xy(o)
        mine = whole.at[pl.ds(32 * core + place, 2)]
        return remote(mine, mine, hxy_send.at[o], hxy_recv.at[o], x=to_x, y=to_y)

    def back_c():
        return remote(whole.at[half], whole.at[half], gc_sem.at[2], gc_sem.at[3], c=1 - core)

    term_c().start()
    term_c().wait_recv()
    share_c[...] = share_c[...] + share[half]
    each(1, 16, lambda o: term_xy(o).start())
    each(1, 16, lambda o: term_xy(o).wait_recv())
    total = share_c[pl.ds(place, 2)]
    for o in range(1, 16):
        total += share_xy[o]
    share_xy[0] = total
    share_z[z] = total
    each(1, 8, lambda o: term_z(o).start())
    each(1, 8, lambda o: term_z(o).wait_recv())
    total = share_z[0]
    for o in range(1, 8):
        total += share_z[o]
    whole[pl.ds(32 * core + place, 2)] = total
    each(1, 16, lambda o: back_xy(o).start())
    each(1, 16, lambda o: back_xy(o).wait_recv())
    back_c().start()
    back_c().wait_recv()
    term_ref[:, :128] = whole[0:32].reshape(256, 128)
    term_ref[:, 128:] = whole[32:64].reshape(256, 128)
    each(1, 16, lambda o: term_xy(o).wait_send())
    each(1, 8, lambda o: term_z(o).wait_send())
    each(1, 16, lambda o: back_xy(o).wait_send())
    three_copy.wait()
    term_c().wait_send()
    back_c().wait_send()
    for l in range(2):
        for h in range(PIECES):
            for n in range(6):
                along_x(l, n, h).wait_send()
            for d in range(3):
                for q in range(2):
                    along_y(l, d, q, h).wait_send()
        for h in range(2):
            to_partner(l, h).wait_send()
        each(1, 7, lambda n: send_sum(l, n).wait_send())
        for s in range(2):
            sum_out(l, s).wait_send()
            sum_on(l, s).wait_send()
    each(1, 16, lambda o: send_index(o).wait_send())
    packs(lambda o: send_pack(o).wait_send())
    for s in range(2):
        pack_out(s).wait_send()
        pack_on(s).wait_send()
    for copy in new_copies:
        copy.wait_send()


def whole_step(*args):
    dma = pltpu.SemaphoreType.DMA
    return pl.pallas_call(
        step_kernel,
        out_shape=(
            jax.ShapeDtypeStruct((1024, 256), BF),
            jax.ShapeDtypeStruct((32, 128, 256), BF),
            jax.ShapeDtypeStruct((256, 256), F32),
        ),
        in_specs=[sspec()] * 5 + [vspec()] * 3 + [aspec()] * 6,
        out_specs=(aspec(), aspec(), vspec()),
        scratch_shapes=[
            VMEM((2, 3, 4, 8, 128, 256), BF),
            VMEM((32, 128, 256), BF),
            VMEM((32, 128, 256), BF),
            VMEM((8, 128, 256), BF),
            VMEM((1024, 256), BF),
            VMEM((1024, 256), BF),
            VMEM((8192, 128), F32),
            VMEM((256, 128), F32),
            VMEM((2, 16, 512, 256), BF),
            VMEM((16, 128, 512), BF),
            VMEM((16, 128, 512), BF),
            VMEM((16, 8, 128), jnp.int32),
            VMEM((16, 8, 128), jnp.int32),
            SMEM((16, 8, 128), jnp.int32),
            VMEM((96, 128, 128), BF),
            VMEM((2, 8, 128, 256), F32),
            VMEM((8, 256, 256), F32),
            VMEM((2, 8, 256, 256), BF),
            VMEM((2, 8, 256, 256), BF),
            VMEM((2, 16, 128, 256), BF),
            VMEM((16, 128, 256), BF),
            VMEM((16, 128, 256), BF),
            VMEM((8, 128, 256), BF),
            VMEM((1024, 256), BF),
            VMEM((1024, 256), BF),
            VMEM((64, 8, 128), F32),
            VMEM((32, 8, 128), F32),
            VMEM((16, 2, 8, 128), F32),
            VMEM((8, 2, 8, 128), F32),
            VMEM((64, 8, 128), F32),
            VMEM((2, 128, 512), BF),
            VMEM((2, 2, 128, 256), BF),
            dma((2, 6, PIECES)), dma((2, 6, PIECES)), dma((2, 6, PIECES)), dma((2, 6, PIECES)),
            dma((16,)), dma((16,)), dma((16,)), dma((16,)),
            dma((2, 2)), dma((2, 2)), dma((2, 8)), dma((2, 8)), dma((3,)), dma((3,)), dma((8,)),
            dma((3, 2)), dma((3, 2)), dma((4,)), dma((16,)), dma((16,)), dma((8,)), dma((8,)),
            dma((16,)), dma((16,)),
        ],
        compiler_params=pltpu.CompilerParams(
            vmem_limit_bytes=60 * MIB, collective_id=1, has_side_effects=True
        ),
        cost_estimate=cost(60e9, 40e6),
    )(*args)


def local(
    h_zero, h_prev, hist_a, hist_b, tile_vals, tile_cols, pull_rows, pull_counts,
    weight_two, weight_three, grad_out,
):
    tile_of, first, near, slots = tables(tile_cols)
    outs = whole_step(
        tile_of, first, near, slots, pull_counts, pull_rows.reshape(64, 128),
        weight_two, weight_three, hist_a.reshape(32, 128, 256), hist_b.reshape(32, 128, 256),
        tile_vals.reshape(96, 128, 128), h_prev.reshape(8, 128, 256), h_zero, grad_out,
    )
    layer_three, fresh_rows, grad_total = published(*outs)
    return (layer_three, fresh_rows.reshape(4096, 256), grad_total)


def solution(mesh):
    finer = Mesh(mesh.devices.reshape(8, 4, 2, mesh.shape["rep"]), (Z, X, C, Y))
    return jax.shard_map(
        local,
        mesh=finer,
        in_specs=(
            P(DEV_REP, None),
            P(DEV_REP, None),
            P(DEV, None),
            P(DEV, None),
            P(DEV_REP, None, None, None),
            P(DEV_REP, None),
            P(DEV_REP, None, None),
            P(DEV_REP, None),
            P(),
            P(),
            P(DEV_REP, None),
        ),
        out_specs=(P(DEV_REP, None), P(DEV, None), P()),
        check_vma=False,
    )
```

time: 191 us -> 157 us (0.82)
  local copies, waits for them, and re-layouts: 15.1 us -> 0 us
  Pallas kernels: 171 us -> 157 us
  other arithmetic: 3.88 us -> 0 us
    pallas_call x1, Pallas kernels: 169 us -> 152 us  [whole_step(): pl.pallas_call(step_kernel, out_shape=(jax.ShapeDtypeStruct((1024, 256),...]
    unnamed x11 -> x0, local copies, waits for them, and re-layouts: 9.7 us -> none
    gather x5 -> x0, local copies, waits for them, and re-layouts: 3.68 us -> none  [the longest x1 1.43 us: local(): cnt = jnp.take(pull_counts[0], owner)]
    pallas_call x1 -> x2, Pallas kernels: 1.86 us -> 5.11 us  [the longest x1 3.21 us: published(): pl.pallas_call(functools.partial(publish_kernel, n), out_shape=shapes, in...]
    sub x2 -> x0, other arithmetic: 2.05 us -> none  [the longest x1 1.29 us: local(): near = tile_cols[:, :4] - jnp.array([0, 8, 8, 8], dtype=jnp.int32)]
where the time goes in v3:
time: 157 us
  Pallas kernels  157 us (100%)
    pallas_call x1, Pallas kernels, whole_step(): pl.pallas_call(step_kernel, out_shape=(jax.ShapeDtypeStruct((1024, 256),...  152 us
    pallas_call x1, Pallas kernels, published(): pl.pallas_call(functools.partial(publish_kernel, n), out_shape=shapes, in...  3.21 us

profile of v3, /device:TPU:1, one launch (start us, length us, event | category | flops | bytes accessed | tf_op | source)
XLA Modules:
  0.0 157.3 jit_solution(3805015119836925818)
XLA Ops:
  0.6 1.9 %shard_map.130 = (s32[64]{0:T(128)}, s32[64]{0:T(128)}, s32[8,4]{1,0:T(8,128)}, s32[8,2]{1,0:T(8,128)}) custom-call(s32[8,12]{1,0:T(8,128)} %cols_ref.1), custom_call_target="tpu_custom_call" | custom-call | tf_op jit(solution)/shard_map/pallas_call | solution.py:72
  2.5 151.5 %shard_map.131 = (bf16[1024,256]{1,0:T(8,128)(2,1)}, bf16[32,128,256]{2,1,0:T(8,128)(2,1)}, f32[256,256]{1,0:T(8,128)}) custom-call(s32[64]{0:T(128)} %get-tuple-element.13.tile_ref, s32[64]{0:T(128)} %get-tuple-element.14.first_ref, s32[8,4]{1,0:T(8,128)} %get-tuple-element.15.cols_ref, s32[8,2]{1,0:T(8,128)} %get-tuple-element.16.from_ref, ...), custom_call_target="tpu_custom_call" | custom-call | flops 60000002048 | bytes 40000000 | tf_op jit(solution)/shard_map/pallas_call | solution.py:591
  154.1 3.2 %shard_map.132 = (bf16[1024,256]{1,0:T(8,128)(2,1)}, bf16[32,128,256]{2,1,0:T(8,128)(2,1)}, f32[256,256]{1,0:T(8,128)}) custom-call(bf16[1024,256]{1,0:T(8,128)(2,1)} %get-tuple-element.17.refs_0_, bf16[32,128,256]{2,1,0:T(8,128)(2,1)} %get-tuple-element.18.refs_1_, f32[256,256]{1,0:T(8,128)} %get-tuple-element.19.refs_2_), custom_call_target="tpu_custom_call" | custom-call | flops 1000000 | bytes 6000000 | tf_op jit(solution)/shard_map/pallas_call | solution.py:99

commit v4 on v3

--- a/solution.py
+++ b/solution.py
@@ -15,6 +15,7 @@
 AXES = {"z": Z, "x": X, "c": C, "y": Y}
 MIB = 1024 * 1024
 PIECES = 4
+WIDTHS = (256, 128, 128)
 
 restart = 0.1
 strength = 0.5
@@ -115,17 +116,23 @@
     tile_ref, first_ref, cols_ref, from_ref, cnt_ref, pull_ref, weight_two_ref, weight_three_ref,
     hist_a_ref, hist_b_ref, tiles_hbm, prev_hbm, zero_hbm, grad_hbm,
     three_ref, fresh_ref, term_ref,
-    far, own_a, own_b, prev_ref, zero_ref, grad_ref, table, got, rows, pack_ref, vin, idx_ref, idx_in,
-    idx, tiles, home, same, other, partner, sums,
-    arrived_a, arrived_b, second, low, three, share, share_c, share_xy, share_z, whole, v_mid, s_mid,
-    far_send, far_recv, y_send, y_recv, idx_send, idx_recv, v_send, v_recv,
-    pair_send, pair_recv, sum_send, sum_recv, new_send, new_recv, local_sem,
-    far_z_send, far_z_recv, gc_sem, gxy_send, gxy_recv, gz_send, gz_recv, hxy_send, hxy_recv,
+    *refs,
 ):
+    refs = iter(refs)
+    far, rows, same, other, partner, sums, s_mid, arrived = (
+        [next(refs) for _ in range(3)] for _ in range(8)
+    )
+    (
+        own_a, own_b, prev_ref, zero_ref, grad_ref, table, got, pack_ref, vin, idx_ref, idx_in,
+        idx, tiles, home, second, low, three, share, share_c, share_xy, share_z, whole, v_mid,
+        far_send, far_recv, y_send, y_recv, idx_send, idx_recv, v_send, v_recv,
+        pair_send, pair_recv, sum_send, sum_recv, new_send, new_recv, local_sem,
+        far_z_send, far_z_recv, gc_sem, gxy_send, gxy_recv, gz_send, gz_recv, hxy_send, hxy_recv,
+    ) = refs
     z, x, core, turn = (lax.axis_index(a) for a in (Z, X, C, Y))
     hist = (hist_a_ref, hist_b_ref)
     own = (own_a, own_b)
-    arrived = (arrived_a, arrived_b)
+    layer = (0, 1, 1)
 
     def remote(src, dst, send, recv, **to):
         return pltpu.make_async_remote_copy(
@@ -188,7 +195,7 @@
     down, up = rem(x + 3, 4), rem(x + 1, 4)
 
     def piece(l, d, q, h):
-        return far.at[l, d, q, pl.ds(h * size, size)]
+        return far[l].at[d, q, pl.ds(h * size, size)]
 
     def along_x(l, n, h):
         d, q, relayed, to = (
@@ -196,7 +203,9 @@
             (1, 0, (0, 0), down), (1, 1, (2, 1), up),
         )[n]
         if relayed is None:
-            src = hist[l].at[pl.ds(rem(turn + q, 4) * 8 + h * size, size)]
+            src = hist[layer[l]].at[pl.ds(rem(turn + q, 4) * 8 + h * size, size)]
+            if l:
+                src = src.at[:, :, pl.ds(128 * (l - 1), 128)]
         else:
             src = piece(l, *relayed, h)
         return remote(
@@ -256,13 +265,13 @@
 
     def sum_out(l, s):
         return remote(
-            sums.at[l, s], s_mid.at[l, s],
+            sums[l].at[s], s_mid[l].at[s],
             far_z_send.at[1 + l, s], far_z_recv.at[1 + l, s], z=rem(z + (1, 7)[s], 8),
         )
 
     def sum_on(l, s):
         return remote(
-            s_mid.at[l, s], arrived[l].at[s],
+            s_mid[l].at[s], arrived[l].at[s],
             sum_send.at[l, 7 * s], sum_recv.at[l, 7 * s], z=rem(z + (3, 5)[s], 8),
         )
 
@@ -303,22 +312,32 @@
         def widen(s, carry):
             r = pl.multiple_of(s * 128, 128)
             if d == 0:
-                block = own[l][rem(s + 8 * turn, 32)]
+                block = own[layer[l]][rem(s + 8 * turn, 32)]
+                if l:
+                    block = block[:, 128 * (l - 1) : 128 * l]
             else:
-                block = far[l, d - 1, s // 8, lax.rem(s, 8)]
+                block = far[l][d - 1, s // 8, lax.rem(s, 8)]
             block = block.astype(F32)
-            table[pl.ds(2 * r, 128, stride=2), :] = block[:, :128]
-            table[pl.ds(2 * r + 1, 128, stride=2), :] = block[:, 128:]
+            if l:
+                table[pl.ds(r, 128), :] = block
+            else:
+                table[pl.ds(2 * r, 128, stride=2), :] = block[:, :128]
+                table[pl.ds(2 * r + 1, 128, stride=2), :] = block[:, 128:]
             return carry
 
         lax.fori_loop(0, 32, widen, 0)
 
         def worker(g):
-            for j in range(128):
-                got[pl.ds(2 * j, 2), :] = table[pl.ds(2 * idx[g, d, j], 2), :]
-            left, right = got[pl.ds(0, 128, stride=2), :], got[pl.ds(1, 128, stride=2), :]
-            both = jnp.concatenate([left, right], axis=1).astype(BF)
-            rows[l, g, pl.ds(d * 128, 128), :] = both
+            if l:
+                for j in range(128):
+                    got[pl.ds(j, 1), :] = table[pl.ds(idx[g, d, j], 1), :]
+                both = got[0:128, :].astype(BF)
+            else:
+                for j in range(128):
+                    got[pl.ds(2 * j, 2), :] = table[pl.ds(2 * idx[g, d, j], 2), :]
+                left, right = got[pl.ds(0, 128, stride=2), :], got[pl.ds(1, 128, stride=2), :]
+                both = jnp.concatenate([left, right], axis=1).astype(BF)
+            rows[l][g, pl.ds(d * 128, 128), :] = both
 
         each(0, 16, worker)
 
@@ -331,40 +350,40 @@
         flag = jnp.concatenate([idx_in[g, 4 + d : 5 + d, :] for d in range(4)], axis=1)
         flag = flag.astype(F32).astype(BF)
         both = jnp.concatenate([packed * flag, packed * (1 - flag)], axis=0)
-        return jnp.dot(both, rows[l, g], preferred_element_type=F32)
+        return jnp.dot(both, rows[l][g], preferred_element_type=F32)
 
     def to_partner(l, h):
         part = pl.ds(4 * h, 4)
         return remote(
-            other.at[l, part], partner.at[l, part], pair_send.at[l, h], pair_recv.at[l, h],
+            other[l].at[part], partner[l].at[part], pair_send.at[l, h], pair_recv.at[l, h],
             c=1 - core,
         )
 
     def send_sum(l, n):
         return remote(
-            sums.at[l, pl.ds(2 * n, 2)], arrived[l].at[pl.ds(2 * n, 2)], sum_send.at[l, n], sum_recv.at[l, n],
+            sums[l].at[pl.ds(2 * n, 2)], arrived[l].at[pl.ds(2 * n, 2)], sum_send.at[l, n], sum_recv.at[l, n],
             z=rem(z + away(n), 8),
         )
 
     def plane_sums(l):
         for h in range(2):
             def for_partner(n):
-                other[l, n] = product(l, n, 1 - core).astype(BF)
+                other[l][n] = product(l, n, 1 - core).astype(BF)
 
             each(4 * h, 4 * h + 4, for_partner)
             if h:
                 to_partner(l, 0).start()
 
         def for_me(n):
-            same[n] = product(l, n, core)
+            same[l][n] = product(l, n, core)
 
         each(0, 4, for_me)
         to_partner(l, 1).start()
         each(4, 8, for_me)
 
         def add(n):
-            both = (same[n] + partner[l, n].astype(F32)).astype(BF)
-            sums[l, pl.ds(2 * n, 2)] = both.reshape(2, 128, 256)
+            both = (same[l][n] + partner[l][n].astype(F32)).astype(BF)
+            sums[l][pl.ds(2 * n, 2)] = both.reshape(2, 128, both.shape[1])
 
         to_partner(l, 0).wait_recv()
         add(0)
@@ -394,8 +413,11 @@
 
     def finish(l, i):
         mine = pl.ds(pl.multiple_of(i * 128, 128), 128)
-        total = home[l, i] + arrived[l][from_ref[i, 0]].astype(F32)
-        total += arrived[l][from_ref[i, 1]].astype(F32)
+        parts = [
+            arrived[st][from_ref[i, 0]].astype(F32) + arrived[st][from_ref[i, 1]].astype(F32)
+            for st in range(3) if layer[st] == l
+        ]
+        total = home[l, i] + (parts[0] if l == 0 else jnp.concatenate(parts, axis=1))
         mixed = (1.0 - restart) * total + restart * zero_ref[mine, :].astype(F32)
         factor = math.log(strength / (l + 2) + 1.0)
         rounded = mixed.astype(BF)
@@ -430,65 +452,93 @@
 
     for copy in local_copies:
         copy.wait()
+    relay(0)
+    own_rows(1)
     each(1, 16, lambda o: send_index(o).wait_recv())
     to_smem = pltpu.make_async_copy(idx_in, idx, local_sem.at[5])
     to_smem.start()
     to_smem.wait()
-    relay(0)
-    own_rows(1)
     gather(0, 0)
     at_home(0)
     pass_packs()
     second_pair(0)
     gather(1, 0)
+    gather(2, 0)
     third_pair(0)
     y_here(0, 0)
     gather(0, 1)
     y_here(0, 2)
     gather(0, 3)
     relay(1)
+    own_rows(2)
     y_here(0, 1)
     gather(0, 2)
+    second_pair(1)
     packs(lambda o: send_pack(o).wait_recv())
     for s in range(2):
         pack_on(s).wait_recv()
     plane_sums(0)
-    second_pair(1)
+    third_pair(1)
     at_home(1)
     pass_sums(0)
-    third_pair(1)
     y_here(1, 0)
     gather(1, 1)
+    relay(2)
     y_here(1, 2)
     gather(1, 3)
+    second_pair(2)
     y_here(1, 1)
     gather(1, 2)
     plane_sums(1)
-    arrived_a[14:16] = sums[0, 14:16]
+    third_pair(2)
+    y_here(2, 0)
+    gather(2, 1)
+    y_here(2, 2)
+    gather(2, 3)
+    pass_sums(1)
+    y_here(2, 1)
+    gather(2, 2)
+    plane_sums(2)
+    for st in range(3):
+        arrived[st][14:16] = sums[st][14:16]
     arrived_here(0)
 
     def layer_two(i):
         second[i] = finish(0, i)[2]
 
     each(0, 8, layer_two)
-    pass_sums(1)
-    plane = fresh_ref.at[pl.ds(turn * 8, 8)]
-    new_copies = [
-        remote(second, plane, new_send.at[s - 1], new_recv.at[s - 1], y=rem(turn + s, 4))
-        for s in (1, 2, 3)
-    ]
-    for copy in new_copies:
-        copy.start()
-    keep = pltpu.make_async_copy(second, plane, local_sem.at[6])
-    keep.start()
 
     def add_current(i):
         block = second[cols_ref[i, 0]]
         home[1, i] += jnp.dot(tiles[12 * i], block, preferred_element_type=F32)
 
     each(0, 8, add_current)
-    arrived_b[14:16] = sums[1, 14:16]
+    keep = pltpu.make_async_copy(second, fresh_ref.at[pl.ds(turn * 8, 8)], local_sem.at[6])
+    keep.start()
+
+    def new_rows(way, h, on):
+        at = rem(turn + (0 if not on else (3, 1)[way]), 4) * 8 + 4 * h
+        there = fresh_ref.at[pl.ds(at, 4)]
+        here = there if on else second.at[pl.ds(4 * h, 4)]
+        n = 3 * way + (2 if on else h)
+        return remote(here, there, new_send.at[n], new_recv.at[n], y=rem(turn + (1, 3)[way], 4))
+
+    def new_here(way, n):
+        at = rem(turn + (2 if n == 2 else (3, 1)[way]), 4) * 8 + 4 * (way if n == 2 else n)
+        half = fresh_ref.at[pl.ds(at, 4)]
+        remote(
+            half, half, new_send.at[3 * way], new_recv.at[3 * way + n], y=rem(turn + 1, 4)
+        ).wait_recv()
+
+    for h in range(2):
+        for way in range(2):
+            new_rows(way, (h, 1 - h)[way], False).start()
+    pass_sums(2)
+    for way in range(2):
+        new_here(way, way)
+        new_rows(way, way, True).start()
     arrived_here(1)
+    arrived_here(2)
 
     def layer_three(i):
         mine, rounded, out = finish(1, i)
@@ -503,9 +553,6 @@
     share[0:32] = term[:, :128].reshape(32, 8, 128)
     share[32:64] = term[:, 128:].reshape(32, 8, 128)
     three_copy.start()
-    for copy in new_copies:
-        copy.wait_recv()
-    keep.wait()
 
     half, theirs = pl.ds(32 * core, 32), pl.ds(32 * (1 - core), 32)
     place = 2 * (4 * x + turn)
@@ -564,7 +611,7 @@
     three_copy.wait()
     term_c().wait_send()
     back_c().wait_send()
-    for l in range(2):
+    for l in range(3):
         for h in range(PIECES):
             for n in range(6):
                 along_x(l, n, h).wait_send()
@@ -582,8 +629,13 @@
     for s in range(2):
         pack_out(s).wait_send()
         pack_on(s).wait_send()
-    for copy in new_copies:
-        copy.wait_send()
+    keep.wait()
+    for way in range(2):
+        for n in (1 - way, 2):
+            new_here(way, n)
+        for h in range(2):
+            new_rows(way, h, False).wait_send()
+        new_rows(way, way, True).wait_send()
 
 
 def whole_step(*args):
@@ -598,7 +650,14 @@
         in_specs=[sspec()] * 5 + [vspec()] * 3 + [aspec()] * 6,
         out_specs=(aspec(), aspec(), vspec()),
         scratch_shapes=[
-            VMEM((2, 3, 4, 8, 128, 256), BF),
+            *(VMEM((3, 4, 8, 128, w), BF) for w in WIDTHS),
+            *(VMEM((16, 512, w), BF) for w in WIDTHS),
+            *(VMEM((8, 256, w), F32) for w in WIDTHS),
+            *(VMEM((8, 256, w), BF) for w in WIDTHS),
+            *(VMEM((8, 256, w), BF) for w in WIDTHS),
+            *(VMEM((16, 128, w), BF) for w in WIDTHS),
+            *(VMEM((2, 128, w), BF) for w in WIDTHS),
+            *(VMEM((16, 128, w), BF) for w in WIDTHS),
             VMEM((32, 128, 256), BF),
             VMEM((32, 128, 256), BF),
             VMEM((8, 128, 256), BF),
@@ -606,7 +665,6 @@
             VMEM((1024, 256), BF),
             VMEM((8192, 128), F32),
             VMEM((256, 128), F32),
-            VMEM((2, 16, 512, 256), BF),
             VMEM((16, 128, 512), BF),
             VMEM((16, 128, 512), BF),
             VMEM((16, 8, 128), jnp.int32),
@@ -614,12 +672,6 @@
             SMEM((16, 8, 128), jnp.int32),
             VMEM((96, 128, 128), BF),
             VMEM((2, 8, 128, 256), F32),
-            VMEM((8, 256, 256), F32),
-            VMEM((2, 8, 256, 256), BF),
-            VMEM((2, 8, 256, 256), BF),
-            VMEM((2, 16, 128, 256), BF),
-            VMEM((16, 128, 256), BF),
-            VMEM((16, 128, 256), BF),
             VMEM((8, 128, 256), BF),
             VMEM((1024, 256), BF),
             VMEM((1024, 256), BF),
@@ -629,15 +681,14 @@
             VMEM((8, 2, 8, 128), F32),
             VMEM((64, 8, 128), F32),
             VMEM((2, 128, 512), BF),
-            VMEM((2, 2, 128, 256), BF),
-            dma((2, 6, PIECES)), dma((2, 6, PIECES)), dma((2, 6, PIECES)), dma((2, 6, PIECES)),
+            *(dma((3, 6, PIECES)) for _ in range(4)),
             dma((16,)), dma((16,)), dma((16,)), dma((16,)),
-            dma((2, 2)), dma((2, 2)), dma((2, 8)), dma((2, 8)), dma((3,)), dma((3,)), dma((8,)),
-            dma((3, 2)), dma((3, 2)), dma((4,)), dma((16,)), dma((16,)), dma((8,)), dma((8,)),
+            dma((3, 2)), dma((3, 2)), dma((3, 8)), dma((3, 8)), dma((6,)), dma((6,)), dma((8,)),
+            dma((4, 2)), dma((4, 2)), dma((4,)), dma((16,)), dma((16,)), dma((8,)), dma((8,)),
             dma((16,)), dma((16,)),
         ],
         compiler_params=pltpu.CompilerParams(
-            vmem_limit_bytes=60 * MIB, collective_id=1, has_side_effects=True
+            vmem_limit_bytes=63 * MIB, collective_id=1, has_side_effects=True
         ),
         cost_estimate=cost(60e9, 40e6),
     )(*args)

time: 157 us -> 150 us (0.955)
  Pallas kernels: 157 us -> 149 us
    pallas_call x1, Pallas kernels: 152 us -> 144 us  [whole_step(): pl.pallas_call(step_kernel, out_shape=(jax.ShapeDtypeStruct((1024, 256),...]
where the time goes in v4:
time: 150 us
  Pallas kernels  149 us (99%)
    pallas_call x1, Pallas kernels, whole_step(): pl.pallas_call(step_kernel, out_shape=(jax.ShapeDtypeStruct((1024, 256),...  144 us
    pallas_call x1, Pallas kernels, published(): pl.pallas_call(functools.partial(publish_kernel, n), out_shape=shapes, in...  3.21 us

profile of v4, /device:TPU:1, one launch (start us, length us, event | category | flops | bytes accessed | tf_op | source)
XLA Modules:
  0.0 149.8 jit_solution(17102655294748048191)
XLA Ops:
  0.6 1.9 %shard_map.130 = (s32[64]{0:T(128)}, s32[64]{0:T(128)}, s32[8,4]{1,0:T(8,128)}, s32[8,2]{1,0:T(8,128)}) custom-call(s32[8,12]{1,0:T(8,128)} %cols_ref.1), custom_call_target="tpu_custom_call" | custom-call | tf_op jit(solution)/shard_map/pallas_call | solution.py:73
  2.5 144.0 %shard_map.131 = (bf16[1024,256]{1,0:T(8,128)(2,1)}, bf16[32,128,256]{2,1,0:T(8,128)(2,1)}, f32[256,256]{1,0:T(8,128)}) custom-call(s32[64]{0:T(128)} %get-tuple-element.13.tile_ref, s32[64]{0:T(128)} %get-tuple-element.14.first_ref, s32[8,4]{1,0:T(8,128)} %get-tuple-element.15.cols_ref, s32[8,2]{1,0:T(8,128)} %get-tuple-element.16.from_ref, ...), custom_call_target="tpu_custom_call" | custom-call | flops 60000002048 | bytes 40000000 | tf_op jit(solution)/shard_map/pallas_call | solution.py:643
  146.6 3.2 %shard_map.132 = (bf16[1024,256]{1,0:T(8,128)(2,1)}, bf16[32,128,256]{2,1,0:T(8,128)(2,1)}, f32[256,256]{1,0:T(8,128)}) custom-call(bf16[1024,256]{1,0:T(8,128)(2,1)} %get-tuple-element.17.refs_0_, bf16[32,128,256]{2,1,0:T(8,128)(2,1)} %get-tuple-element.18.refs_1_, f32[256,256]{1,0:T(8,128)} %get-tuple-element.19.refs_2_), custom_call_target="tpu_custom_call" | custom-call | flops 1000000 | bytes 6000000 | tf_op jit(solution)/shard_map/pallas_call | solution.py:100

commit v5 on v4

--- a/solution.py
+++ b/solution.py
@@ -165,8 +165,6 @@
     ]
     tiles_copy = pltpu.make_async_copy(tiles_hbm, tiles, local_sem.at[2])
     tiles_copy.start()
-    for copy in local_copies:
-        copy.start()
 
     def owner(g, d):
         return 8 * (g // 2) + 2 * lax.rem(x + d, 4) + lax.rem(g, 2)
@@ -183,13 +181,13 @@
 
     lane = lax.broadcasted_iota(jnp.int32, (128, 128), 1)
 
-    def pack(g, carry):
+    def pack(o):
+        g = 2 * rem(z + o // 2, 8) + rem(core + o % 2, 2)
         for d in range(4):
             p = owner(g, d)
             tile = tiles[tile_ref[p]].astype(F32)
             tile = jnp.where(lane < cnt_ref[0, p], tile, 0.0).astype(BF)
             pack_ref[g, :, d * 128 : (d + 1) * 128] = tile
-        return carry
 
     size = 8 // PIECES
     down, up = rem(x + 3, 4), rem(x + 1, 4)
@@ -209,26 +207,34 @@
         else:
             src = piece(l, *relayed, h)
         return remote(
-            src, piece(l, d, q, h), far_send.at[l, n, h], far_recv.at[l, 2 * d + q, h], x=to
+            src, piece(l, d, q, h), far_send.at[l, n], far_recv.at[l, 2 * d + q, h], x=to
         )
 
     def along_y(l, d, q, h):
         to, at = (rem(turn + 1, 4), 3) if q == 0 else (rem(turn + 3, 4), 2)
         return remote(
             piece(l, d, q, h), piece(l, d, at, h),
-            y_send.at[l, 2 * d + q, h], y_recv.at[l, 2 * d + q, h], y=to,
+            y_send.at[l, 2 * d + q], y_recv.at[l, 2 * d + q], y=to,
         )
 
     def x_here(l, d, q, h):
         remote(
             piece(l, d, q, h), piece(l, d, q, h),
-            far_send.at[l, 0, h], far_recv.at[l, 2 * d + q, h], x=down,
+            far_send.at[l, 0], far_recv.at[l, 2 * d + q, h], x=down,
         ).wait_recv()
+
+    def whole_y(l, d, q):
+        to, at = (rem(turn + 1, 4), 3) if q == 0 else (rem(turn + 3, 4), 2)
+        return remote(
+            far[l].at[d, q], far[l].at[d, at], y_send.at[l, 2 * d + q], y_recv.at[l, 2 * d + q], y=to
+        )
+
+    def whole_x(l, n):
+        return remote(far[l].at[0, 0], far[l].at[0, 0], far_send.at[l, n], far_recv.at[l, 0, 0], x=up)
 
     def y_here(l, d):
         for q in range(2):
-            for h in range(PIECES):
-                along_y(l, d, q, h).wait_recv()
+            whole_y(l, d, q).wait_recv()
 
     def own_rows(l):
         for n in (0, 2, 1, 3):
@@ -301,12 +307,26 @@
     own_rows(0)
     each(1, 16, lambda o: send_index(o).start())
     tiles_copy.wait()
-    lax.fori_loop(0, 16, pack, 0)
+
+    def pack_and_send(o):
+        pack(o)
+        send_pack(o - 1).start()
+
+    pack(8)
+    pack(9)
+    pack_out(0).start()
+    pack(10)
+    pack_out(1).start()
+    each(11, 16, pack_and_send)
+    pack(1)
+    send_pack(15).start()
+    each(2, 8, pack_and_send)
+    pack(0)
+    send_pack(7).start()
+    for copy in local_copies:
+        copy.start()
     idx_in[2 * z + core] = idx_ref[2 * z + core]
     vin[2 * z + core] = pack_ref[2 * z + core]
-    for s in range(2):
-        pack_out(s).start()
-    packs(lambda o: send_pack(o).start())
 
     def gather(l, d):
         def widen(s, carry):
@@ -467,23 +487,23 @@
     third_pair(0)
     y_here(0, 0)
     gather(0, 1)
+    relay(1)
+    own_rows(2)
     y_here(0, 2)
     gather(0, 3)
-    relay(1)
-    own_rows(2)
+    second_pair(1)
     y_here(0, 1)
     gather(0, 2)
-    second_pair(1)
     packs(lambda o: send_pack(o).wait_recv())
     for s in range(2):
         pack_on(s).wait_recv()
     plane_sums(0)
     third_pair(1)
     at_home(1)
+    relay(2)
     pass_sums(0)
     y_here(1, 0)
     gather(1, 1)
-    relay(2)
     y_here(1, 2)
     gather(1, 3)
     second_pair(2)
@@ -612,12 +632,11 @@
     term_c().wait_send()
     back_c().wait_send()
     for l in range(3):
-        for h in range(PIECES):
-            for n in range(6):
-                along_x(l, n, h).wait_send()
-            for d in range(3):
-                for q in range(2):
-                    along_y(l, d, q, h).wait_send()
+        for n in range(6):
+            whole_x(l, n).wait_send()
+        for d in range(3):
+            for q in range(2):
+                whole_y(l, d, q).wait_send()
         for h in range(2):
             to_partner(l, h).wait_send()
         each(1, 7, lambda n: send_sum(l, n).wait_send())
@@ -681,7 +700,7 @@
             VMEM((8, 2, 8, 128), F32),
             VMEM((64, 8, 128), F32),
             VMEM((2, 128, 512), BF),
-            *(dma((3, 6, PIECES)) for _ in range(4)),
+            dma((3, 6)), dma((3, 6, PIECES)), dma((3, 6)), dma((3, 6)),
             dma((16,)), dma((16,)), dma((16,)), dma((16,)),
             dma((3, 2)), dma((3, 2)), dma((3, 8)), dma((3, 8)), dma((6,)), dma((6,)), dma((8,)),
             dma((4, 2)), dma((4, 2)), dma((4,)), dma((16,)), dma((16,)), dma((8,)), dma((8,)),

time: 150 us -> 147 us (0.980)
  Pallas kernels: 149 us -> 146 us
    pallas_call x1, Pallas kernels: 144 us -> 141 us  [whole_step(): pl.pallas_call(step_kernel, out_shape=(jax.ShapeDtypeStruct((1024, 256),...]
where the time goes in v5:
time: 147 us
  Pallas kernels  146 us (99%)
    pallas_call x1, Pallas kernels, whole_step(): pl.pallas_call(step_kernel, out_shape=(jax.ShapeDtypeStruct((1024, 256),...  141 us
    pallas_call x1, Pallas kernels, published(): pl.pallas_call(functools.partial(publish_kernel, n), out_shape=shapes, in...  3.21 us

profile of v5, /device:TPU:1, one launch (start us, length us, event | category | flops | bytes accessed | tf_op | source)
XLA Modules:
  0.0 146.8 jit_solution(11633567797085108650)
XLA Ops:
  0.6 1.9 %shard_map.130 = (s32[64]{0:T(128)}, s32[64]{0:T(128)}, s32[8,4]{1,0:T(8,128)}, s32[8,2]{1,0:T(8,128)}) custom-call(s32[8,12]{1,0:T(8,128)} %cols_ref.1), custom_call_target="tpu_custom_call" | custom-call | tf_op jit(solution)/shard_map/pallas_call | solution.py:73
  2.5 141.0 %shard_map.131 = (bf16[1024,256]{1,0:T(8,128)(2,1)}, bf16[32,128,256]{2,1,0:T(8,128)(2,1)}, f32[256,256]{1,0:T(8,128)}) custom-call(s32[64]{0:T(128)} %get-tuple-element.13.tile_ref, s32[64]{0:T(128)} %get-tuple-element.14.first_ref, s32[8,4]{1,0:T(8,128)} %get-tuple-element.15.cols_ref, s32[8,2]{1,0:T(8,128)} %get-tuple-element.16.from_ref, ...), custom_call_target="tpu_custom_call" | custom-call | flops 60000002048 | bytes 40000000 | tf_op jit(solution)/shard_map/pallas_call | solution.py:662
  143.6 3.2 %shard_map.132 = (bf16[1024,256]{1,0:T(8,128)(2,1)}, bf16[32,128,256]{2,1,0:T(8,128)(2,1)}, f32[256,256]{1,0:T(8,128)}) custom-call(bf16[1024,256]{1,0:T(8,128)(2,1)} %get-tuple-element.17.refs_0_, bf16[32,128,256]{2,1,0:T(8,128)(2,1)} %get-tuple-element.18.refs_1_, f32[256,256]{1,0:T(8,128)} %get-tuple-element.19.refs_2_), custom_call_target="tpu_custom_call" | custom-call | flops 1000000 | bytes 6000000 | tf_op jit(solution)/shard_map/pallas_call | solution.py:100
